TPU v7x, 16 devices: a whole 2x2x2 slice. The times are simulated.
16 devices in a mesh: dp: 2 (over z), sp: 8 (over y, x, core).
Axes of the slice: x: 2, y: 2, z: 2, core: 2. Of those that a mesh axis runs over, the one named last changes fastest.
Arguments:
- hidden: bfloat16 [6, 2048, 512], P('dp', 'sp')
- grad_out: bfloat16 [6, 2048, 512], P('dp', 'sp')
- ln1_gain: float32 [512], replicated
- ln1_bias: float32 [512], replicated
- ln2_gain: float32 [512], replicated
- ln2_bias: float32 [512], replicated
- w_qkv: bfloat16 [512, 8, 3, 64], replicated
- b_qkv: float32 [1536], replicated
- w_dense: bfloat16 [512, 512], replicated
- b_dense: float32 [512], replicated
- w_in: bfloat16 [512, 2048], replicated
- b_in: float32 [2048], replicated
- w_out: bfloat16 [2048, 512], replicated
- b_out: float32 [512], replicated
Outputs:
- output 1: bfloat16 [6, 2048, 512], P('dp', 'sp')
- output 2: bfloat16 [6, 2048, 512], P('dp', 'sp')
- output 3: float32 [512], P(('dp', 'sp'))
- output 4: float32 [512], P(('dp', 'sp'))
- output 5: float32 [512], P(('dp', 'sp'))
- output 6: float32 [512], P(('dp', 'sp'))
- output 7: float32 [512, 8, 3, 64], P(('dp', 'sp'))
- output 8: float32 [1536], P(('dp', 'sp'))
- output 9: float32 [512, 512], P(('dp', 'sp'))
- output 10: float32 [512], P(('dp', 'sp'))
- output 11: float32 [512, 2048], P(('dp', 'sp'))
- output 12: float32 [2048], P(('dp', 'sp'))
- output 13: float32 [2048, 512], P(('dp', 'sp'))
- output 14: float32 [512], P(('dp', 'sp'))
All inputs are finite; a program needn't handle non-finite values.
Results may differ from a plain program's by a relative error of at most 0.0105531.
Values are sent between devices in bfloat16 or wider.
A program may use at most 1 GiB of HBM per device.

v0:
```python
import math
import jax
import jax.numpy as jnp
from jax import lax
from jax.sharding import PartitionSpec as P

LN_EPS = 1e-5
ROPE_BASE = 10000.0


def norm_fwd(x_f32, ln_gain, ln_shift):
    mean_val = jnp.mean(x_f32, axis=-1, keepdims=True)
    centered = x_f32 - mean_val
    var_val = jnp.mean(centered * centered, axis=-1, keepdims=True)
    inv_std = lax.rsqrt(var_val + LN_EPS)
    x_hat = centered * inv_std
    return (x_hat * ln_gain + ln_shift).astype(jnp.bfloat16), x_hat, inv_std


def norm_bwd(d_norm, x_hat, inv_std, ln_gain):
    d_gain = jnp.sum(d_norm * x_hat, axis=(0, 1))
    d_shift = jnp.sum(d_norm, axis=(0, 1))
    d_hat = d_norm * ln_gain
    d_input = inv_std * (d_hat - jnp.mean(d_hat, axis=-1, keepdims=True) - x_hat * jnp.mean(d_hat * x_hat, axis=-1, keepdims=True))
    return d_input, d_gain, d_shift


def rope_tables(positions, rot_dim):
    inv_freq = ROPE_BASE ** (-jnp.arange(0, rot_dim, 2, dtype=jnp.float32) / rot_dim)
    angles = positions.astype(jnp.float32)[:, None] * inv_freq[None, :]
    angles = jnp.concatenate([angles, angles], axis=-1)[:, None, :]
    return jnp.cos(angles), jnp.sin(angles)


def rotate(x_f32, cos_t, sin_t, rot_dim):
    half_rot = rot_dim // 2
    x_rot = x_f32[..., :rot_dim]
    turned = jnp.concatenate([-x_rot[..., half_rot:], x_rot[..., :half_rot]], axis=-1)
    return jnp.concatenate([x_rot * cos_t + turned * sin_t, x_f32[..., rot_dim:]], axis=-1)


def rotate_back(d_f32, cos_t, sin_t, rot_dim):
    half_rot = rot_dim // 2
    d_rot = d_f32[..., :rot_dim]
    scaled = d_rot * sin_t
    turned = jnp.concatenate([-scaled[..., half_rot:], scaled[..., :half_rot]], axis=-1)
    return jnp.concatenate([d_rot * cos_t - turned, d_f32[..., rot_dim:]], axis=-1)


def query_block(n_batch, n_heads, seq_len):
    max_rows = min(512, max(8, (1 << 22) // (n_batch * n_heads * seq_len)))
    q_blk = 8
    for step_num in range(6):
        if q_blk * 2 <= max_rows and seq_len % (q_blk * 2) == 0:
            q_blk = q_blk * 2
    return q_blk


def attend_fwd(q_all, k_all, v_all, q_blk):
    seq_len = q_all.shape[1]
    attn_scale = 1.0 / math.sqrt(q_all.shape[3])
    key_pos = jnp.arange(seq_len)

    def one_block(blk_index):
        q_start = blk_index * q_blk
        q_part = lax.dynamic_slice_in_dim(q_all, q_start, q_blk, axis=1)
        scores = jnp.einsum('bqhe,bkhe->bhqk', q_part, k_all, preferred_element_type=jnp.float32) * attn_scale
        causal = key_pos[None, :] <= (q_start + jnp.arange(q_blk))[:, None]
        attn_prob = jax.nn.softmax(jnp.where(causal, scores, -1e30), axis=-1)
        return jnp.einsum('bhqk,bkhe->bqhe', attn_prob.astype(jnp.bfloat16), v_all, preferred_element_type=jnp.float32).astype(jnp.bfloat16)

    blocks = lax.map(one_block, jnp.arange(seq_len // q_blk))
    return jnp.moveaxis(blocks, 0, 1).reshape(q_all.shape)


def attend_bwd(q_all, k_all, v_all, d_ctx, q_blk):
    seq_len = q_all.shape[1]
    attn_scale = 1.0 / math.sqrt(q_all.shape[3])
    key_pos = jnp.arange(seq_len)

    def one_block(acc_pair, blk_index):
        dk_acc, dv_acc = acc_pair
        q_start = blk_index * q_blk
        q_part = lax.dynamic_slice_in_dim(q_all, q_start, q_blk, axis=1)
        dc_part = lax.dynamic_slice_in_dim(d_ctx, q_start, q_blk, axis=1)
        scores = jnp.einsum('bqhe,bkhe->bhqk', q_part, k_all, preferred_element_type=jnp.float32) * attn_scale
        causal = key_pos[None, :] <= (q_start + jnp.arange(q_blk))[:, None]
        attn_prob = jax.nn.softmax(jnp.where(causal, scores, -1e30), axis=-1)
        d_prob = jnp.einsum('bqhe,bkhe->bhqk', dc_part, v_all, preferred_element_type=jnp.float32)
        d_score = attn_prob * (d_prob - jnp.sum(d_prob * attn_prob, axis=-1, keepdims=True)) * attn_scale
        ds_bf = d_score.astype(jnp.bfloat16)
        dq_part = jnp.einsum('bhqk,bkhe->bqhe', ds_bf, k_all, preferred_element_type=jnp.float32).astype(jnp.bfloat16)
        dk_acc = dk_acc + jnp.einsum('bhqk,bqhe->bkhe', ds_bf, q_part, preferred_element_type=jnp.float32)
        dv_acc = dv_acc + jnp.einsum('bhqk,bqhe->bkhe', attn_prob.astype(jnp.bfloat16), dc_part, preferred_element_type=jnp.float32)
        return (dk_acc, dv_acc), dq_part

    zero_acc = jnp.zeros(q_all.shape, jnp.float32)
    acc_pair, dq_blocks = lax.scan(one_block, (zero_acc, zero_acc), jnp.arange(seq_len // q_blk))
    d_query = jnp.moveaxis(dq_blocks, 0, 1).reshape(q_all.shape)
    return d_query, acc_pair[0].astype(jnp.bfloat16), acc_pair[1].astype(jnp.bfloat16)


def solution(mesh):
    sp_size = mesh.shape['sp']
    grad_axes = ('dp', 'sp')

    def to_heads(tensor):
        return lax.all_to_all(tensor, 'sp', 2, 1, tiled=True)

    def to_tokens(tensor):
        return lax.all_to_all(tensor, 'sp', 1, 2, tiled=True)

    def device_step(hidden, grad_out, ln1_gain, ln1_bias, ln2_gain, ln2_bias, w_qkv, b_qkv, w_dense, b_dense, w_in, b_in, w_out, b_out):
        n_batch, n_tok, d_model = hidden.shape
        n_heads = w_qkv.shape[1]
        head_dim = w_qkv.shape[3]
        rot_dim = head_dim // 4
        q_blk = query_block(n_batch, n_heads // sp_size, n_tok * sp_size)
        positions = lax.axis_index('sp') * n_tok + jnp.arange(n_tok)
        cos_t, sin_t = rope_tables(positions, rot_dim)

        hidden_f32 = hidden.astype(jnp.float32)
        h_attn, hat_attn, inv_attn = norm_fwd(hidden_f32, ln1_gain, ln1_bias)
        h_mlp, hat_mlp, inv_mlp = norm_fwd(hidden_f32, ln2_gain, ln2_bias)
        qkv_proj = jnp.einsum('btd,dhce->bthce', h_attn, w_qkv, preferred_element_type=jnp.float32) + b_qkv.reshape(n_heads, 3, head_dim)
        q_heads = to_heads(rotate(qkv_proj[:, :, :, 0], cos_t, sin_t, rot_dim).astype(jnp.bfloat16))
        k_heads = to_heads(rotate(qkv_proj[:, :, :, 1], cos_t, sin_t, rot_dim).astype(jnp.bfloat16))
        v_heads = to_heads(qkv_proj[:, :, :, 2].astype(jnp.bfloat16))
        ctx_heads = attend_fwd(q_heads, k_heads, v_heads, q_blk)
        ctx_tok = to_tokens(ctx_heads).reshape(n_batch, n_tok, d_model)
        attn_out = jnp.einsum('btc,ce->bte', ctx_tok, w_dense, preferred_element_type=jnp.float32) + b_dense
        pre_act = jnp.einsum('btd,df->btf', h_mlp, w_in, preferred_element_type=jnp.float32) + b_in
        act_bf = jax.nn.gelu(pre_act, approximate=False).astype(jnp.bfloat16)
        mlp_out = jnp.einsum('btf,fe->bte', act_bf, w_out, preferred_element_type=jnp.float32) + b_out
        out_hidden = (hidden_f32 + attn_out + mlp_out).astype(jnp.bfloat16)

        grad_f32 = grad_out.astype(jnp.float32)
        g_b_dense = jnp.sum(grad_f32, axis=(0, 1))
        g_w_dense = jnp.einsum('btc,bte->ce', ctx_tok, grad_out, preferred_element_type=jnp.float32)
        g_w_out = jnp.einsum('btf,bte->fe', act_bf, grad_out, preferred_element_type=jnp.float32)
        d_ctx = jnp.einsum('bte,ce->btc', grad_out, w_dense, preferred_element_type=jnp.float32).astype(jnp.bfloat16).reshape(n_batch, n_tok, n_heads, head_dim)
        d_act = jnp.einsum('bte,fe->btf', grad_out, w_out, preferred_element_type=jnp.float32)
        gauss_cdf = 0.5 * (1.0 + lax.erf(pre_act * math.sqrt(0.5)))
        gauss_pdf = jnp.exp(-0.5 * pre_act * pre_act) * (1.0 / math.sqrt(2.0 * math.pi))
        d_pre = d_act * (gauss_cdf + pre_act * gauss_pdf)
        d_pre_bf = d_pre.astype(jnp.bfloat16)
        g_b_in = jnp.sum(d_pre, axis=(0, 1))
        g_w_in = jnp.einsum('btd,btf->df', h_mlp, d_pre_bf, preferred_element_type=jnp.float32)
        d_h_mlp = jnp.einsum('btf,df->btd', d_pre_bf, w_in, preferred_element_type=jnp.float32)

        dq_heads, dk_heads, dv_heads = attend_bwd(q_heads, k_heads, v_heads, to_heads(d_ctx), q_blk)
        dq_tok = rotate_back(to_tokens(dq_heads).astype(jnp.float32), cos_t, sin_t, rot_dim)
        dk_tok = rotate_back(to_tokens(dk_heads).astype(jnp.float32), cos_t, sin_t, rot_dim)
        dv_tok = to_tokens(dv_heads).astype(jnp.float32)
        d_qkv = jnp.stack([dq_tok, dk_tok, dv_tok], axis=3)
        d_qkv_bf = d_qkv.astype(jnp.bfloat16)
        g_b_qkv = jnp.sum(d_qkv, axis=(0, 1)).reshape(-1)
        g_w_qkv = jnp.einsum('btd,bthce->dhce', h_attn, d_qkv_bf, preferred_element_type=jnp.float32)
        d_h_attn = jnp.einsum('bthce,dhce->btd', d_qkv_bf, w_qkv, preferred_element_type=jnp.float32)
        dx_attn, g_ln1_gain, g_ln1_bias = norm_bwd(d_h_attn, hat_attn, inv_attn, ln1_gain)
        dx_mlp, g_ln2_gain, g_ln2_bias = norm_bwd(d_h_mlp, hat_mlp, inv_mlp, ln2_gain)
        grad_hidden = (grad_f32 + dx_attn + dx_mlp).astype(jnp.bfloat16)

        local_grads = [g_ln1_gain, g_ln1_bias, g_ln2_gain, g_ln2_bias, g_w_qkv, g_b_qkv, g_w_dense, g_b_dense, g_w_in, g_b_in, g_w_out]
        summed = [lax.psum_scatter(part_sum, grad_axes, scatter_dimension=0, tiled=True) for part_sum in local_grads]
        return tuple([out_hidden, grad_hidden] + summed + [summed[7]])

    tok_spec = P('dp', 'sp', None)
    grad_spec = P(grad_axes)
    return jax.shard_map(device_step, mesh=mesh, in_specs=(tok_spec, tok_spec) + (P(),) * 12, out_specs=(tok_spec, tok_spec) + (grad_spec,) * 12, check_vma=False)
```

profile of v0, /device:TPU:0, one launch (start us, length us, event | category | flops | bytes accessed | tf_op | source)
XLA Modules:
  0.0 774.0 jit_solution(3869598380746020734)
XLA Ops:
  20.5 5.5 all-to-all-start.1
  28.4 10.2 %all-to-all-done.1 = bf16[3,256,8,64]{1,3,0,2:T(8,128)(2,1)S(1)} async-done(((bf16[3,256,8,64]{1,3,0,2:T(8,128)(2,1)}), bf16[3,256,8,64]{1,3,0,2:T(8,128)(2,1)S(1)}, u32[]{:S(2)}, u32[]{:S(2)}) %all-to-all-start.1) | async-done | bytes 786464 | tf_op jit(solution)/shard_map/all_to_all | solution.py:108
  38.5 4.2 all-to-all-start
  45.2 10.0 %all-to-all-done = bf16[3,256,8,64]{1,3,0,2:T(8,128)(2,1)} async-done(((bf16[3,256,8,64]{1,3,0,2:T(8,128)(2,1)}), bf16[3,256,8,64]{1,3,0,2:T(8,128)(2,1)}, u32[]{:S(2)}, u32[]{:S(2)}) %all-to-all-start) | async-done | bytes 786464 | tf_op jit(solution)/shard_map/all_to_all | solution.py:108
  55.2 4.2 all-to-all-start.2
  66.4 5.4 all-to-all-done.2
  71.9 4.2 all-to-all-start.4
  80.4 8.1 %all-to-all-done.4 = bf16[3,256,8,64]{1,3,0,2:T(8,128)(2,1)} async-done(((bf16[3,256,8,64]{1,3,0,2:T(8,128)(2,1)}), bf16[3,256,8,64]{1,3,0,2:T(8,128)(2,1)}, u32[]{:S(2)}, u32[]{:S(2)}) %all-to-all-start.4) | async-done | bytes 786464 | tf_op jit(solution)/shard_map/all_to_all | solution.py:108
  91.6 278.3 %while.27 = (s32[]{:T(128)}, f32[3,2048,1,64]{1,3,0,2:T(8,128)}, f32[3,2048,1,64]{1,3,0,2:T(8,128)}, bf16[4,3,512,1,64]{2,4,1,3,0:T(8,128)(2,1)}, s32[4]{0:T(128...) while((s32[]{:T(128)}, f32[3,2048,1,64]{1,3,0,2:T(8,128)}, ...), condition=%wide.region_10.11_spmd.clone, body=%wide.region_6.10_spmd.clone.sunk | while | flops 2078909952 | bytes 150192848 | solution.py:98
  94.7 10.3 %fusion.258 = (f32[3,512]{1,0:T(4,128)S(1)}, f32[3,512,2048]{2,1,0:T(8,128)}) fusion(pred[512,2048]{1,0:T(8,128)(4,1)} %iota_compare_fusion.5, bf16[3,2048,1,64]{1,3,0,2:T(8,128)(2,1)} %get-tuple-element.470, bf16[3,2048,1,64]{1,3,0,2:T(8,128)(2,1)} %get-tuple-element.469, s32[]{:T(128)S(6)} %select_n.47), kind=kOutput, calls=%fused_computation.218.clone.1 | convolution fusion | flops 415238144 | bytes 14620676 | tf_op jit(solution)/shard_map/while/body/eval_jaxpr/sub | solution.py:88
  105.0 7.3 fusion.257
  112.3 19.9 %fusion.261 = bf16[4,3,512,1,64]{2,4,1,3,0:T(8,128)(2,1)} fusion(bf16[4,3,512,1,64]{2,4,1,3,0:T(8,128)(2,1)} %get-tuple-element.454, s32[]{:T(128)} %get-tuple-element.451, f32[3,512,2048]{2,1,0:T(8,128)} %fusion.257, bf16[3,2048,1,64]{1,3,0,2:T(8,128)(2,1)} %get-tuple-element.470, f32[3,512,2048]{2,1,0:T(8,128)} %get-tuple-element.406, ...), kind=kOutput, calls=%fused_computation.53.clone.1 | convolution fusion | flops 424775168 | bytes 51331584 | tf_op jit(solution)/shard_map/while/body/eval_jaxpr/bhqk,bkhe->bqhe/dot_general | solution.py:92
  132.1 7.2 fusion.260
  139.3 21.2 %fusion.259 = f32[3,2048,1,64]{1,3,0,2:T(8,128)} fusion(f32[3,512,2048]{2,1,0:T(8,128)} %fusion.257, f32[3,2048,1,64]{1,3,0,2:T(8,128)} %get-tuple-element.452, pred[]{:T(512)S(6)} %compare.3, bf16[3,2048,1,64]{1,3,0,2:T(8,128)(2,1)} %get-tuple-element.469, s32[]{:T(128)S(6)} %select_n.47, f32[3,512,2048]{2,1,0:T(8,128)} %get-tuple-element.406, ...), kind=kOutput, calls=%fused_computation.49.clone.1 | convolution fusion | flops 425463296 | bytes 53690372 | tf_op jit(solution)/shard_map/while/body/eval_jaxpr/bhqk,bqhe->bkhe/dot_general | solution.py:93
  163.5 10.3 %fusion.258 = (f32[3,512]{1,0:T(4,128)S(1)}, f32[3,512,2048]{2,1,0:T(8,128)}) fusion(pred[512,2048]{1,0:T(8,128)(4,1)} %iota_compare_fusion.5, bf16[3,2048,1,64]{1,3,0,2:T(8,128)(2,1)} %get-tuple-element.470, bf16[3,2048,1,64]{1,3,0,2:T(8,128)(2,1)} %get-tuple-element.469, s32[]{:T(128)S(6)} %select_n.47), kind=kOutput, calls=%fused_computation.218.clone.1 | convolution fusion | flops 415238144 | bytes 14620676 | tf_op jit(solution)/shard_map/while/body/eval_jaxpr/sub | solution.py:88
  173.7 7.3 fusion.257
  181.0 19.9 %fusion.261 = bf16[4,3,512,1,64]{2,4,1,3,0:T(8,128)(2,1)} fusion(bf16[4,3,512,1,64]{2,4,1,3,0:T(8,128)(2,1)} %get-tuple-element.454, s32[]{:T(128)} %get-tuple-element.451, f32[3,512,2048]{2,1,0:T(8,128)} %fusion.257, bf16[3,2048,1,64]{1,3,0,2:T(8,128)(2,1)} %get-tuple-element.470, f32[3,512,2048]{2,1,0:T(8,128)} %get-tuple-element.406, ...), kind=kOutput, calls=%fused_computation.53.clone.1 | convolution fusion | flops 424775168 | bytes 51331584 | tf_op jit(solution)/shard_map/while/body/eval_jaxpr/bhqk,bkhe->bqhe/dot_general | solution.py:92
  200.9 7.6 fusion.260
  208.5 21.7 %fusion.259 = f32[3,2048,1,64]{1,3,0,2:T(8,128)} fusion(f32[3,512,2048]{2,1,0:T(8,128)} %fusion.257, f32[3,2048,1,64]{1,3,0,2:T(8,128)} %get-tuple-element.452, pred[]{:T(512)S(6)} %compare.3, bf16[3,2048,1,64]{1,3,0,2:T(8,128)(2,1)} %get-tuple-element.469, s32[]{:T(128)S(6)} %select_n.47, f32[3,512,2048]{2,1,0:T(8,128)} %get-tuple-element.406, ...), kind=kOutput, calls=%fused_computation.49.clone.1 | convolution fusion | flops 425463296 | bytes 53690372 | tf_op jit(solution)/shard_map/while/body/eval_jaxpr/bhqk,bqhe->bkhe/dot_general | solution.py:93
  233.1 10.3 %fusion.258 = (f32[3,512]{1,0:T(4,128)S(1)}, f32[3,512,2048]{2,1,0:T(8,128)}) fusion(pred[512,2048]{1,0:T(8,128)(4,1)} %iota_compare_fusion.5, bf16[3,2048,1,64]{1,3,0,2:T(8,128)(2,1)} %get-tuple-element.470, bf16[3,2048,1,64]{1,3,0,2:T(8,128)(2,1)} %get-tuple-element.469, s32[]{:T(128)S(6)} %select_n.47), kind=kOutput, calls=%fused_computation.218.clone.1 | convolution fusion | flops 415238144 | bytes 14620676 | tf_op jit(solution)/shard_map/while/body/eval_jaxpr/sub | solution.py:88
  243.4 7.3 fusion.257
  250.7 19.9 %fusion.261 = bf16[4,3,512,1,64]{2,4,1,3,0:T(8,128)(2,1)} fusion(bf16[4,3,512,1,64]{2,4,1,3,0:T(8,128)(2,1)} %get-tuple-element.454, s32[]{:T(128)} %get-tuple-element.451, f32[3,512,2048]{2,1,0:T(8,128)} %fusion.257, bf16[3,2048,1,64]{1,3,0,2:T(8,128)(2,1)} %get-tuple-element.470, f32[3,512,2048]{2,1,0:T(8,128)} %get-tuple-element.406, ...), kind=kOutput, calls=%fused_computation.53.clone.1 | convolution fusion | flops 424775168 | bytes 51331584 | tf_op jit(solution)/shard_map/while/body/eval_jaxpr/bhqk,bkhe->bqhe/dot_general | solution.py:92
  270.6 7.6 fusion.260
  278.2 21.7 %fusion.259 = f32[3,2048,1,64]{1,3,0,2:T(8,128)} fusion(f32[3,512,2048]{2,1,0:T(8,128)} %fusion.257, f32[3,2048,1,64]{1,3,0,2:T(8,128)} %get-tuple-element.452, pred[]{:T(512)S(6)} %compare.3, bf16[3,2048,1,64]{1,3,0,2:T(8,128)(2,1)} %get-tuple-element.469, s32[]{:T(128)S(6)} %select_n.47, f32[3,512,2048]{2,1,0:T(8,128)} %get-tuple-element.406, ...), kind=kOutput, calls=%fused_computation.49.clone.1 | convolution fusion | flops 425463296 | bytes 53690372 | tf_op jit(solution)/shard_map/while/body/eval_jaxpr/bhqk,bqhe->bkhe/dot_general | solution.py:93
  302.8 10.3 %fusion.258 = (f32[3,512]{1,0:T(4,128)S(1)}, f32[3,512,2048]{2,1,0:T(8,128)}) fusion(pred[512,2048]{1,0:T(8,128)(4,1)} %iota_compare_fusion.5, bf16[3,2048,1,64]{1,3,0,2:T(8,128)(2,1)} %get-tuple-element.470, bf16[3,2048,1,64]{1,3,0,2:T(8,128)(2,1)} %get-tuple-element.469, s32[]{:T(128)S(6)} %select_n.47), kind=kOutput, calls=%fused_computation.218.clone.1 | convolution fusion | flops 415238144 | bytes 14620676 | tf_op jit(solution)/shard_map/while/body/eval_jaxpr/sub | solution.py:88
  313.0 7.3 fusion.257
  320.3 19.9 %fusion.261 = bf16[4,3,512,1,64]{2,4,1,3,0:T(8,128)(2,1)} fusion(bf16[4,3,512,1,64]{2,4,1,3,0:T(8,128)(2,1)} %get-tuple-element.454, s32[]{:T(128)} %get-tuple-element.451, f32[3,512,2048]{2,1,0:T(8,128)} %fusion.257, bf16[3,2048,1,64]{1,3,0,2:T(8,128)(2,1)} %get-tuple-element.470, f32[3,512,2048]{2,1,0:T(8,128)} %get-tuple-element.406, ...), kind=kOutput, calls=%fused_computation.53.clone.1 | convolution fusion | flops 424775168 | bytes 51331584 | tf_op jit(solution)/shard_map/while/body/eval_jaxpr/bhqk,bkhe->bqhe/dot_general | solution.py:92
  340.2 7.6 fusion.260
  347.8 21.7 %fusion.259 = f32[3,2048,1,64]{1,3,0,2:T(8,128)} fusion(f32[3,512,2048]{2,1,0:T(8,128)} %fusion.257, f32[3,2048,1,64]{1,3,0,2:T(8,128)} %get-tuple-element.452, pred[]{:T(512)S(6)} %compare.3, bf16[3,2048,1,64]{1,3,0,2:T(8,128)(2,1)} %get-tuple-element.469, s32[]{:T(128)S(6)} %select_n.47, f32[3,512,2048]{2,1,0:T(8,128)} %get-tuple-element.406, ...), kind=kOutput, calls=%fused_computation.49.clone.1 | convolution fusion | flops 425463296 | bytes 53690372 | tf_op jit(solution)/shard_map/while/body/eval_jaxpr/bhqk,bqhe->bkhe/dot_general | solution.py:93
  376.3 4.2 reshape.295
  380.5 4.2 all-to-all-start.6
  384.8 4.0 copy.153
  388.8 4.2 reshape.297
  393.0 4.2 all-to-all-done.6
  397.2 4.2 all-to-all-start.5
  403.8 4.0 copy.132
  407.8 4.2 reshape.293
  412.0 4.1 reshape.296
  423.7 4.2 all-to-all-start.7
  427.9 4.2 reshape.298
  441.7 4.2 reshape.294
  456.0 5.3 convolution_bitcast_fusion.2
  462.3 82.2 %while.26 = (s32[]{:T(128)}, bf16[4,3,512,1,64]{2,4,1,3,0:T(8,128)(2,1)}, s32[4]{0:T(128)S(1)}, bf16[3,2048,1,64]{1,3,0,2:T(8,128)(2,1)}, bf16[3,2048,1,64]{1,3,...) while((s32[]{:T(128)}, ...), condition=%wide.region_5.6_spmd.clone, body=%wide.region_2.5_spmd.clone.sunk | while | flops 825330176 | bytes 29246120 | solution.py:72
  465.4 10.2 %fusion.245 = (f32[3,512]{1,0:T(4,128)S(1)}, f32[3,512,2048]{2,1,0:T(8,128)}) fusion(pred[512,2048]{1,0:T(8,128)(4,1)} %iota_compare_fusion.4, bf16[3,2048,1,64]{1,3,0,2:T(8,128)(2,1)} %get-tuple-element.432, bf16[3,2048,1,64]{1,3,0,2:T(8,128)(2,1)} %get-tuple-element.431, s32[]{:T(128)S(6)} %select_n.45), kind=kOutput, calls=%fused_computation.217.clone.1 | convolution fusion | flops 415238144 | bytes 14620676 | tf_op jit(solution)/shard_map/while/body/eval_jaxpr/sub | solution.py:69
  475.6 7.3 fusion.246
  485.9 10.2 %fusion.245 = (f32[3,512]{1,0:T(4,128)S(1)}, f32[3,512,2048]{2,1,0:T(8,128)}) fusion(pred[512,2048]{1,0:T(8,128)(4,1)} %iota_compare_fusion.4, bf16[3,2048,1,64]{1,3,0,2:T(8,128)(2,1)} %get-tuple-element.432, bf16[3,2048,1,64]{1,3,0,2:T(8,128)(2,1)} %get-tuple-element.431, s32[]{:T(128)S(6)} %select_n.45), kind=kOutput, calls=%fused_computation.217.clone.1 | convolution fusion | flops 415238144 | bytes 14620676 | tf_op jit(solution)/shard_map/while/body/eval_jaxpr/sub | solution.py:69
  496.1 7.3 fusion.246
  506.4 10.2 %fusion.245 = (f32[3,512]{1,0:T(4,128)S(1)}, f32[3,512,2048]{2,1,0:T(8,128)}) fusion(pred[512,2048]{1,0:T(8,128)(4,1)} %iota_compare_fusion.4, bf16[3,2048,1,64]{1,3,0,2:T(8,128)(2,1)} %get-tuple-element.432, bf16[3,2048,1,64]{1,3,0,2:T(8,128)(2,1)} %get-tuple-element.431, s32[]{:T(128)S(6)} %select_n.45), kind=kOutput, calls=%fused_computation.217.clone.1 | convolution fusion | flops 415238144 | bytes 14620676 | tf_op jit(solution)/shard_map/while/body/eval_jaxpr/sub | solution.py:69
  516.7 7.3 fusion.246
  526.9 10.2 %fusion.245 = (f32[3,512]{1,0:T(4,128)S(1)}, f32[3,512,2048]{2,1,0:T(8,128)}) fusion(pred[512,2048]{1,0:T(8,128)(4,1)} %iota_compare_fusion.4, bf16[3,2048,1,64]{1,3,0,2:T(8,128)(2,1)} %get-tuple-element.432, bf16[3,2048,1,64]{1,3,0,2:T(8,128)(2,1)} %get-tuple-element.431, s32[]{:T(128)S(6)} %select_n.45), kind=kOutput, calls=%fused_computation.217.clone.1 | convolution fusion | flops 415238144 | bytes 14620676 | tf_op jit(solution)/shard_map/while/body/eval_jaxpr/sub | solution.py:69
  537.2 7.3 fusion.246
  544.5 4.1 copy.150
  548.6 4.2 reshape.291
  552.8 4.2 all-to-all-start.3
  557.2 6.6 fusion.170
  563.7 5.8 all-to-all-done.3
  569.5 4.2 reshape.292
  580.7 15.9 %fusion.116 = bf16[3,256,2048]{2,1,0:T(8,128)(2,1)S(1)} fusion(f32[3,256,2048]{2,1,0:T(8,128)} %get-tuple-element.300, f32[2048]{0:T(1024)S(1)} %copy-done.34, u8[256,2048]{1,0:T(8,128)(4,1)} %get-tuple-element.226, u8[256,2048]{1,0:T(8,128)(4,1)S(1)} %get-tuple-element.225), kind=kLoop, calls=%fused_computation.86 | loop fusion | flops 111673344 | bytes 10493952 | tf_op jit(solution)/shard_map/convert_element_type | solution.py:133
  602.1 6.5 fusion.206
  614.4 5.1 fusion.134
  622.9 5.6 fusion.160
  630.4 33.2 %all-reduce.7 = (f32[512]{0:T(512)S(1)}, f32[512]{0:T(512)S(1)}, f32[512]{0:T(512)S(1)}, f32[512]{0:T(512)S(1)}, f32[1536]{0:T(1024)S(1)}, /*index=5*/f32[512]{0:T(512)S(1)}, f32[2048]{0:T(1024)S(1)}) all-reduce(f32[512]{0:T(512)S(1)} %get-tuple-element.229, ...), channel_id=2, replica_groups=mesh['dp'=2,'sp'=8] {'dp','sp'}, use_global_device_ids=true, to_apply=%region_16.17.clone | all-reduce | flops 6144 | bytes 49152
  672.5 28.0 %reduce-scatter.11.cloned.1.call-done = f32[128,512]{1,0:T(8,128)} async-done(((f32[2048,512]{1,0:T(8,128)}), f32[128,512]{1,0:T(8,128)}) %reduce-scatter.11.cloned.1.call-update) | async-done | bytes 262160 | tf_op jit(solution)/shard_map/reduce_scatter | solution.py:165
  700.6 66.2 %reduce-scatter.9.cloned.1.call-done = f32[32,2048]{1,0:T(8,128)} async-done(((f32[512,2048]{1,0:T(8,128)}), f32[32,2048]{1,0:T(8,128)}) %reduce-scatter.9.cloned.1.call-update) | async-done | bytes 262160 | tf_op jit(solution)/shard_map/reduce_scatter | solution.py:165
  (200 shorter events, 120.2 us)
Async XLA Ops:
  7.2 549.9 %copy-start = (bf16[512,2048]{1,0:T(8,128)(2,1)S(1)}, bf16[512,2048]{1,0:T(8,128)(2,1)}, u32[]{:S(2)}) copy-start(bf16[512,2048]{1,0:T(8,128)(2,1)} %param.28) | copy-start | bytes 6291460
  8.7 5.5 copy-start.24
  10.2 4.0 copy-start.30
  14.3 2.2 copy-start.15
  14.6 2.3 copy-start.11
  14.6 2.7 copy-start.12
  17.5 2.0 copy-start.26
  17.5 2.0 copy-start.28
  19.5 7.8 %copy-start.23 = (bf16[3,256,8,16]{1,3,2,0:T(8,128)(2,1)S(1)}, bf16[3,256,8,16]{1,3,2,0:T(8,128)(2,1)}, u32[]{:S(2)}) copy-start(bf16[3,256,8,16]{1,3,2,0:T(8,128)(2,1)} %get-tuple-element.293) | copy-start | bytes 589828
  20.5 18.0 %all-to-all-start.1 = ((bf16[3,256,8,64]{1,3,0,2:T(8,128)(2,1)}), bf16[3,256,8,64]{1,3,0,2:T(8,128)(2,1)S(1)}, u32[]{:S(2)}, u32[]{:S(2)}) async-start(bf16[3,256,8,64]{1,3,0,2:T(8,128)(2,1)} %copy.111), calls=%async_computation.1 | async-start | bytes 1572864 | tf_op jit(solution)/shard_map/all_to_all | solution.py:108
  28.4 31.0 %copy-start.37 = (bf16[512,512]{1,0:T(8,128)(2,1)S(1)}, bf16[512,512]{1,0:T(8,128)(2,1)}, u32[]{:S(2)}) copy-start(bf16[512,512]{1,0:T(8,128)(2,1)} %param.26) | copy-start | bytes 1572868
  38.5 16.7 %all-to-all-start = ((bf16[3,256,8,64]{1,3,0,2:T(8,128)(2,1)}), bf16[3,256,8,64]{1,3,0,2:T(8,128)(2,1)}, u32[]{:S(2)}, u32[]{:S(2)}) async-start(bf16[3,256,8,64]{1,3,0,2:T(8,128)(2,1)} %copy.109), calls=%async_computation | async-start | bytes 1572864 | tf_op jit(solution)/shard_map/all_to_all | solution.py:108
  55.2 16.7 %all-to-all-start.2 = ((bf16[3,256,8,64]{1,3,0,2:T(8,128)(2,1)}), bf16[3,256,8,64]{1,3,0,2:T(8,128)(2,1)}, u32[]{:S(2)}, u32[]{:S(2)}) async-start(bf16[3,256,8,64]{1,3,0,2:T(8,128)(2,1)} %copy.113), calls=%async_computation.2 | async-start | bytes 1572864 | tf_op jit(solution)/shard_map/all_to_all | solution.py:108
  71.9 16.7 %all-to-all-start.4 = ((bf16[3,256,8,64]{1,3,0,2:T(8,128)(2,1)}), bf16[3,256,8,64]{1,3,0,2:T(8,128)(2,1)}, u32[]{:S(2)}, u32[]{:S(2)}) async-start(bf16[3,256,8,64]{1,3,0,2:T(8,128)(2,1)} %copy.121), calls=%async_computation.4 | async-start | bytes 1572864 | tf_op jit(solution)/shard_map/all_to_all | solution.py:108
  380.5 16.7 %all-to-all-start.6 = ((bf16[8,2,24576]{2,1,0:T(2,128)(2,1)}), bf16[8,2,24576]{2,1,0:T(2,128)(2,1)}, u32[]{:S(2)}, u32[]{:S(2)}) async-start(bf16[8,2,24576]{2,1,0:T(2,128)(2,1)} %reshape.295), calls=%async_computation.6 | async-start | bytes 1572864 | tf_op jit(solution)/shard_map/all_to_all | solution.py:111
  397.2 26.4 %all-to-all-start.5 = ((bf16[8,2,24576]{2,1,0:T(2,128)(2,1)}), bf16[8,2,24576]{2,1,0:T(2,128)(2,1)}, u32[]{:S(2)}, u32[]{:S(2)}) async-start(bf16[8,2,24576]{2,1,0:T(2,128)(2,1)} %reshape.297), calls=%async_computation.5 | async-start | bytes 1572864 | tf_op jit(solution)/shard_map/all_to_all | solution.py:111
  423.7 18.1 %all-to-all-start.7 = ((bf16[8,2,24576]{2,1,0:T(2,128)(2,1)}), bf16[8,2,24576]{2,1,0:T(2,128)(2,1)}, u32[]{:S(2)}, u32[]{:S(2)}) async-start(bf16[8,2,24576]{2,1,0:T(2,128)(2,1)} %reshape.293), calls=%async_computation.7 | async-start | bytes 1572864 | tf_op jit(solution)/shard_map/all_to_all | solution.py:111
  427.9 242.7 %reduce-scatter.5.cloned.1.call-start = ((), (), s32[]{:S(2)}) async-start(), calls=%async_computation.12 | async-start | bytes 6684672 | tf_op jit(solution)/shard_map/reduce_scatter | solution.py:165
  438.0 1.8 copy-start.3
  438.5 2.5 copy-start.4
  438.5 2.4 copy-start.29
  451.1 1.2 copy-start.22
  451.2 1.2 copy-start.27
  451.8 2.4 copy-start.14
  452.3 2.3 copy-start.5
  452.3 2.2 copy-start.13
  454.2 1.8 copy-start.1
  454.2 1.8 copy-start.25
  454.2 1.8 copy-start.31
  454.2 1.8 copy-start.35
  454.3 1.8 copy-start.38
  454.4 1.1 copy-start.7
  454.6 1.4 copy-start.9
  544.5 12.6 %copy-start.2 = (bf16[3,256,512]{2,1,0:T(8,128)(2,1)S(1)}, bf16[3,256,512]{2,1,0:T(8,128)(2,1)}, u32[]{:S(2)}) copy-start(bf16[3,256,512]{2,1,0:T(8,128)(2,1)} %param.18) | copy-start | bytes 2359300
  544.5 12.6 %copy-start.32 = (f32[512]{0:T(512)S(1)}, f32[512]{0:T(512)}, u32[]{:S(2)}) copy-start(f32[512]{0:T(512)} %param.22) | copy-start | bytes 6148
  544.5 12.6 %copy-start.33 = (f32[512]{0:T(512)S(1)}, f32[512]{0:T(512)}, u32[]{:S(2)}) copy-start(f32[512]{0:T(512)} %param.23) | copy-start | bytes 6148
  544.5 12.6 %copy-start.34 = (f32[2048]{0:T(1024)S(1)}, f32[2048]{0:T(1024)}, u32[]{:S(2)}) copy-start(f32[2048]{0:T(1024)} %param.29) | copy-start | bytes 24580
  552.8 16.7 %all-to-all-start.3 = ((bf16[8,2,24576]{2,1,0:T(2,128)(2,1)}), bf16[8,2,24576]{2,1,0:T(2,128)(2,1)}, u32[]{:S(2)}, u32[]{:S(2)}) async-start(bf16[8,2,24576]{2,1,0:T(2,128)(2,1)} %reshape.291), calls=%async_computation.3 | async-start | bytes 1572864 | tf_op jit(solution)/shard_map/all_to_all | solution.py:111
  557.1 115.5 %reduce-scatter.7.cloned.1.call-start = ((), (), s32[]{:S(2)}) async-start(), calls=%async_computation.13 | async-start | bytes 1114112 | tf_op jit(solution)/shard_map/reduce_scatter | solution.py:165
  580.6 120.0 %reduce-scatter.11.cloned.1.call-start = ((), (), s32[]{:S(2)}) async-start(), calls=%async_computation.15 | async-start | bytes 4456448 | tf_op jit(solution)/shard_map/reduce_scatter | solution.py:165
  580.6 17.6 %copy-start.19 = (bf16[3,256,512]{2,1,0:T(8,128)(2,1)S(1)}, bf16[3,256,512]{2,1,0:T(8,128)(2,1)}, u32[]{:S(2)}) copy-start(bf16[3,256,512]{2,1,0:T(8,128)(2,1)} %param.19) | copy-start | bytes 2359300
  596.6 1.7 copy-start.16
  602.1 164.6 %reduce-scatter.9.cloned.1.call-start = ((), (), s32[]{:S(2)}) async-start(), calls=%async_computation.14 | async-start | bytes 4456448 | tf_op jit(solution)/shard_map/reduce_scatter | solution.py:165
  608.6 1.7 copy-start.18
  614.4 5.1 copy-start.17
  614.4 5.1 copy-start.36
  619.5 3.0 copy-start.6
  619.5 3.0 copy-start.8
  619.5 3.0 copy-start.10
  622.8 5.7 copy-start.20
  622.9 5.7 copy-start.21
  628.4 38.7 %copy-start.39 = (f32[512]{0:T(512)S(1)}, f32[512]{0:T(512)}, u32[]{:S(2)}) copy-start(f32[512]{0:T(512)} %param.31) | copy-start | bytes 6148
  628.4 38.7 %copy-start.40 = (f32[512]{0:T(512)S(1)}, f32[512]{0:T(512)}, u32[]{:S(2)}) copy-start(f32[512]{0:T(512)} %param.27) | copy-start | bytes 6148
  663.7 103.6 %copy-start.41 = (f32[32]{0:T(128)}, f32[32]{0:T(128)S(1)}, u32[]{:S(2)}) copy-start(f32[32]{0:T(128)S(1)} %dynamic-slice.5) | copy-start | bytes 388
Sparse Core Ops, SparseCore 0:
  461.5 69.4 reduce-scatter.4
  580.7 54.4 reduce-scatter.6
  638.1 62.4 reduce-scatter.10
  703.3 63.4 reduce-scatter.8
where the time goes:
time: 781 us; the launch traced here: 774 us
  matrix products  388 us (50%)
  waiting for transfers between devices  138 us (18%)
  local copies, waits for them, and re-layouts  110 us (14%)
  other arithmetic  48.4 us (6%)
  starting transfers between devices  35.1 us (4%)
  blocking collectives  33.2 us (4%)
  between operations  14.8 us (2%)
    reduce_scatter x4, waiting for transfers between devices, device_step(): lax.psum_scatter(part_sum, grad_axes, scatter_dimension=0, tiled=True)  94.2 us
    dot_general x4, matrix products, one_block(): jnp.einsum('bhqk,bqhe->bkhe', ds_bf, q_part, preferred_element_type=jnp.f...  86.3 us
    sub x8, matrix products, one_block(): attn_prob = jax.nn.softmax(jnp.where(causal, scores, -1e+30), axis=-1)  82 us
    dot_general x4, matrix products, one_block(): jnp.einsum('bhqk,bkhe->bqhe', ds_bf, k_all, preferred_element_type=jnp.fl...  79.5 us
    unnamed x104, local copies, waits for them, and re-layouts  49 us
    all_to_all x4, waiting for transfers between devices, to_heads(): return lax.all_to_all(tensor, 'sp', 2, 1, tiled=True)  33.7 us
    unnamed x1, blocking collectives  33.2 us
    dot_general x4, matrix products, one_block(): jnp.einsum('bhqk,bqhe->bkhe', attn_prob.astype(jnp.bfloat16), dc_part, pr...  30 us
  transfers between devices with their start and end apart: 12, of which 8 were waited for; matrix products, arithmetic and copies ran while one was open for 29% of the time, Pallas kernels for 0%

commit v1 on v0

v1 whole, which is shorter than its diff:
```python
import math
import jax
import jax.numpy as jnp
from jax import lax
from jax.experimental import pallas as pl
from jax.experimental.pallas import tpu as pltpu
from jax.sharding import PartitionSpec as P

LN_EPS = 1e-5
ROPE_BASE = 10000.0
F32 = jnp.float32
BF16 = jnp.bfloat16
VMEM_LIMIT = 62 * 1024 * 1024

NB, NT, D, NH, HD, FF = 3, 256, 512, 8, 64, 2048
ROWS = NB * NT
SP = 8
SEQ = SP * NT
CHUNK = 512


def dot(a, b):
    return lax.dot_general(a, b, (((1,), (0,)), ((), ())), preferred_element_type=F32)


def dot_tb(a, b):
    return lax.dot_general(a, b, (((1,), (1,)), ((), ())), preferred_element_type=F32)


def lane_iota(rows, cols):
    return lax.broadcasted_iota(jnp.int32, (rows, cols), 1)


def row(ref):
    return ref[...].reshape(1, ref.shape[0])


def layer_hat(x):
    mean_val = jnp.mean(x, axis=-1, keepdims=True)
    centered = x - mean_val
    var_val = jnp.mean(centered * centered, axis=-1, keepdims=True)
    inv_std = lax.rsqrt(var_val + LN_EPS)
    return centered * inv_std, inv_std


def fold_weights(wt_ref, wp_ref):
    for h in range(NH):
        wp_ref[2 * HD * h:2 * HD * (h + 1), :] = wt_ref[3 * HD * h:3 * HD * h + 2 * HD, :]
        wp_ref[2 * D + HD * h:2 * D + HD * (h + 1), :] = wt_ref[3 * HD * h + 2 * HD:3 * HD * (h + 1), :]


def pair_lanes(row_qk, row_v):
    low = lane_iota(row_qk.shape[0], 128) < HD
    tiles = []
    for p in range(NH // 2):
        first = row_qk[:, 256 * p:256 * p + 128]
        second = pltpu.roll(row_qk[:, 256 * p + 128:256 * p + 256], HD, 1)
        v_pair = row_v[:, 128 * p:128 * p + 128]
        tiles += [first, jnp.where(low, v_pair, second), jnp.where(low, second, v_pair)]
    return jnp.concatenate(tiles, axis=1)


def tokens_a(x_ref, g_ref, g1_ref, s1_ref, g2_ref, s2_ref, wt_ref, bqkv_ref, wd_ref, bd_ref, wi_ref, bi_ref, wo_ref, bo_ref,
             cos_ref, sa_ref, sb_ref,
             send_ref, res_ref, dh2_ref, gwot_ref, gwi_ref, gbi_ref, small_ref,
             wp_ref, h2_ref, h2t_ref, gt_ref):
    x = x_ref[...].astype(F32)
    hat, _ = layer_hat(x)
    h1 = (hat * row(g1_ref) + row(s1_ref)).astype(BF16)
    h2_ref[...] = (hat * row(g2_ref) + row(s2_ref)).astype(BF16)
    fold_weights(wt_ref, wp_ref)

    low = lane_iota(NT, 128) < HD
    b_all = row(bqkv_ref)
    for b in range(NB):
        rows = slice(NT * b, NT * (b + 1))
        h_b = h1[rows]
        qk = dot_tb(h_b, wp_ref[:2 * D, :])
        vv = dot_tb(h_b, wp_ref[2 * D:, :])
        dc = dot_tb(g_ref[rows, :], wd_ref[...])
        for p in range(NH // 2):
            bias_a = b_all[:, 384 * p:384 * p + 128]
            bias_m = b_all[:, 384 * p + 128:384 * p + 256]
            bias_c = b_all[:, 384 * p + 256:384 * p + 384]
            low_row = low[:1]
            bias_b = pltpu.roll(jnp.where(low_row, bias_c, bias_m), HD, 1)
            bias_v = jnp.where(low_row, bias_m, bias_c)
            v_pair = vv[:, 128 * p:128 * p + 128] + bias_v
            d_pair = dc[:, 128 * p:128 * p + 128]
            v_turn = pltpu.roll(v_pair, HD, 1)
            d_turn = pltpu.roll(d_pair, HD, 1)
            for h, bias, second in ((2 * p, bias_a, jnp.where(low, v_pair, d_turn)), (2 * p + 1, bias_b, jnp.where(low, v_turn, d_pair))):
                t = qk[:, 128 * h:128 * h + 128] + bias
                t = t * cos_ref[...] + pltpu.roll(t, 120, 1) * sa_ref[...] + pltpu.roll(t, 8, 1) * sb_ref[...]
                send_ref[h, b, :, 0:128] = t.astype(BF16)
                send_ref[h, b, :, 128:256] = second.astype(BF16)

    h2t_ref[...] = h2_ref[...].T
    gt_ref[...] = g_ref[...].T
    g32 = g_ref[...].astype(F32)
    g_b_dense = jnp.sum(g32, axis=0, keepdims=True)
    res_ref[...] = x + row(bd_ref) + row(bo_ref)
    b_in = row(bi_ref)
    for c in range(FF // CHUNK):
        cols = slice(CHUNK * c, CHUNK * (c + 1))
        pre = dot(h2_ref[...], wi_ref[:, cols]) + b_in[:, cols]
        d_act = dot_tb(g_ref[...], wo_ref[cols, :])
        cdf = 0.5 * (1.0 + lax.erf(pre * math.sqrt(0.5)))
        pdf = jnp.exp(-0.5 * pre * pre) * (1.0 / math.sqrt(2.0 * math.pi))
        act = (pre * cdf).astype(BF16)
        d_pre = d_act * (cdf + pre * pdf)
        d_pre_bf = d_pre.astype(BF16)
        gbi_ref[:, cols] = jnp.broadcast_to(jnp.sum(d_pre, axis=0, keepdims=True), (8, CHUNK))
        gwot_ref[:, cols] = dot(gt_ref[...], act)
        gwi_ref[:, cols] = dot(h2t_ref[...], d_pre_bf)
        res_ref[...] += dot(act, wo_ref[cols, :])
        d_h = dot_tb(d_pre_bf, wi_ref[:, cols])
        if c == 0:
            dh2_ref[...] = d_h
        else:
            dh2_ref[...] += d_h
    d_h2 = dh2_ref[...]
    small_ref[...] = jnp.concatenate([jnp.sum(d_h2 * hat, axis=0, keepdims=True), jnp.sum(d_h2, axis=0, keepdims=True), g_b_dense, jnp.zeros((5, D), F32)], axis=0)


def heads_body(in_ref, out_ref, xt_ref, s_ref, dp_ref, acc_ref):
    scale = 1.0 / math.sqrt(HD)
    for j in range(SP):
        xt_ref[:, NT * j:NT * (j + 1)] = in_ref[j, 0].T
    low = lane_iota(NT, 128) < HD
    keep = lax.broadcasted_iota(jnp.int32, (NT, NT), 0) <= lane_iota(NT, NT)
    zero_t = jnp.zeros((HD, NT), BF16)
    for i in reversed(range(SP)):
        cols = slice(NT * i, NT * (i + 1))
        q_t = xt_ref[0:HD, cols] * BF16(scale)
        dc_t = xt_ref[3 * HD:4 * HD, cols]
        w_s = jnp.concatenate([zero_t, q_t, zero_t, zero_t], axis=0)
        w_p = jnp.concatenate([zero_t, zero_t, dc_t, zero_t], axis=0)
        w_sp = jnp.concatenate([w_s, w_p], axis=1)
        q_n = jnp.where(low, in_ref[i, 0, :, 0:128] * BF16(scale), BF16(0.0))
        dc_n = jnp.where(low, BF16(0.0), in_ref[i, 0, :, 128:256])
        w_acc = jnp.concatenate([q_n, dc_n], axis=0)
        top = None
        for j in range(i + 1):
            kv = slice(NT * j, NT * (j + 1))
            both = dot(in_ref[j, 0], w_sp)
            s = both[:, :NT]
            if j == i:
                s = jnp.where(keep, s, -1e30)
            s_ref[kv, :] = s
            dp_ref[kv, :] = both[:, NT:]
            part = jnp.max(s.reshape(NT // 8, 8, NT), axis=0)
            top = part if top is None else jnp.maximum(top, part)
        top = jnp.max(top, axis=0, keepdims=True)
        total = jnp.zeros((8, NT), F32)
        inner = jnp.zeros((8, NT), F32)
        for j in range(i + 1):
            kv = slice(NT * j, NT * (j + 1))
            e = jnp.exp(s_ref[kv, :] - top)
            s_ref[kv, :] = e
            total += jnp.sum(e.reshape(NT // 8, 8, NT), axis=0)
            inner += jnp.sum((e * dp_ref[kv, :]).reshape(NT // 8, 8, NT), axis=0)
        inv = 1.0 / jnp.sum(total, axis=0, keepdims=True)
        delta = jnp.sum(inner, axis=0, keepdims=True) * inv
        ctx_t = jnp.zeros((HD, NT), F32)
        dq_t = jnp.zeros((HD, NT), F32)
        for j in range(i + 1):
            kv = slice(NT * j, NT * (j + 1))
            prob = s_ref[kv, :] * inv
            prob_bf = prob.astype(BF16)
            ds_bf = (prob * (dp_ref[kv, :] - delta)).astype(BF16)
            ctx_t += dot(xt_ref[2 * HD:3 * HD, kv], prob_bf)
            dq_t += dot(xt_ref[HD:2 * HD, kv], ds_bf)
            step = dot(jnp.concatenate([ds_bf, prob_bf], axis=1), w_acc)
            if i == SP - 1:
                acc_ref[kv, :] = step
            else:
                acc_ref[kv, :] += step
        nat = jnp.concatenate([dq_t * scale, ctx_t], axis=0).T
        acc = acc_ref[cols, :]
        out_ref[i, 0, :, 0:128] = jnp.where(low, nat, pltpu.roll(acc, HD, 1)).astype(BF16)
        out_ref[i, 0, :, 128:256] = jnp.where(low, pltpu.roll(nat, HD, 1), acc).astype(BF16)


def tokens_b(z_ref, x_ref, g_ref, res_ref, dh2_ref, gbi_ref, small_ref, g1_ref, s1_ref, g2_ref, wt_ref, wd_ref, cos_ref, sa_ref, sb_ref,
             out_ref, gx_ref, pack_ref,
             wp_ref, ctx_ref, dqkv_ref):
    fold_weights(wt_ref, wp_ref)
    low = lane_iota(NT, 128) < HD
    gb_qk = [None] * NH
    gb_v = [None] * (NH // 2)
    for b in range(NB):
        rows = slice(NT * b, NT * (b + 1))
        for p in range(NH // 2):
            seconds = []
            for h in (2 * p, 2 * p + 1):
                t = z_ref[h, b, :, 0:128].astype(F32)
                t = t * cos_ref[...] - pltpu.roll(t, 120, 1) * sa_ref[...] - pltpu.roll(t, 8, 1) * sb_ref[...]
                part = jnp.sum(t, axis=0, keepdims=True)
                gb_qk[h] = part if b == 0 else gb_qk[h] + part
                dqkv_ref[rows, 128 * h:128 * h + 128] = t.astype(BF16)
                seconds.append(z_ref[h, b, :, 128:256].astype(F32))
            ctx_pair = jnp.where(low, seconds[0], pltpu.roll(seconds[1], HD, 1))
            dv_pair = jnp.where(low, pltpu.roll(seconds[0], HD, 1), seconds[1])
            ctx_ref[rows, 128 * p:128 * p + 128] = ctx_pair.astype(BF16)
            dqkv_ref[rows, 2 * D + 128 * p:2 * D + 128 * p + 128] = dv_pair.astype(BF16)
            part = jnp.sum(dv_pair, axis=0, keepdims=True)
            gb_v[p] = part if b == 0 else gb_v[p] + part
    out_ref[...] = (res_ref[...] + dot(ctx_ref[...], wd_ref[...])).astype(BF16)
    x = x_ref[...].astype(F32)
    hat, inv_std = layer_hat(x)
    h1_t = (hat * row(g1_ref) + row(s1_ref)).astype(BF16).T
    for k in range(3):
        g_qkv = dot(h1_t, dqkv_ref[:, D * k:D * (k + 1)])
        for q in range(16):
            pack_ref[q, 32 * k:32 * k + 32, :] = g_qkv[32 * q:32 * q + 32]
    g_dense = dot(ctx_ref[...].T, g_ref[...])
    for q in range(16):
        pack_ref[q, 96:128, :] = g_dense[32 * q:32 * q + 32]
    d_h1 = dot(dqkv_ref[...], wp_ref[...])
    g_ln1 = jnp.sum(d_h1 * hat, axis=0, keepdims=True)
    g_ln1_b = jnp.sum(d_h1, axis=0, keepdims=True)
    d_hat = d_h1 * row(g1_ref) + dh2_ref[...] * row(g2_ref)
    d_x = inv_std * (d_hat - jnp.mean(d_hat, axis=-1, keepdims=True) - hat * jnp.mean(d_hat * hat, axis=-1, keepdims=True))
    gx_ref[...] = (g_ref[...].astype(F32) + d_x).astype(BF16)

    five = jnp.concatenate([g_ln1, g_ln1_b, small_ref[...][0:3], jnp.zeros((3, D), F32)], axis=0)
    g_bqkv = jnp.broadcast_to(pair_lanes(jnp.concatenate(gb_qk, axis=1), jnp.concatenate(gb_v, axis=1)), (8, 3 * D))
    for q in range(16):
        part = pltpu.roll(five, (D - 32 * q) % D, 1)[:, 0:128] if q else five[:, 0:128]
        bq = pltpu.roll(g_bqkv, (3 * D - 96 * q) % (3 * D), 1)[:, 0:128] if q else g_bqkv[:, 0:128]
        pack_ref[q, 128:136, 0:128] = part
        pack_ref[q, 128:136, 128:256] = gbi_ref[:, 128 * q:128 * q + 128]
        pack_ref[q, 128:136, 256:384] = bq
        pack_ref[q, 128:136, 384:512] = jnp.zeros((8, 128), F32)


def sds(shape, dtype):
    return jax.ShapeDtypeStruct(shape, dtype)


def vmem_specs(count):
    return [pl.BlockSpec(memory_space=pltpu.VMEM)] * count


def solution(mesh):
    grad_axes = ('dp', 'sp')

    def device_step(hidden, grad_out, ln1_gain, ln1_bias, ln2_gain, ln2_bias, w_qkv, b_qkv, w_dense, b_dense, w_in, b_in, w_out, b_out):
        x = hidden.reshape(ROWS, D)
        g = grad_out.reshape(ROWS, D)
        wt = jnp.transpose(w_qkv, (1, 2, 3, 0)).reshape(3 * D, D)
        rot = HD // 4
        half = rot // 2
        lane = jnp.arange(128)
        in_head = lane % HD
        inv_freq = ROPE_BASE ** (-(2.0 * (in_head % half)).astype(F32) / rot)
        pos = (lax.axis_index('sp') * NT + jnp.arange(NT)).astype(F32)
        angles = pos[:, None] * inv_freq[None, :]
        cos_t = jnp.where(in_head[None, :] < rot, jnp.cos(angles), 1.0)
        sin_t = jnp.sin(angles)
        sin_a = jnp.where(in_head[None, :] < half, -sin_t, 0.0)
        sin_b = jnp.where((in_head[None, :] >= half) & (in_head[None, :] < rot), sin_t, 0.0)

        send, res, dh2, gwot, gwi, gbi, small = pl.pallas_call(
            tokens_a,
            out_shape=(sds((SP, NB, NT, 256), BF16), sds((ROWS, D), F32), sds((ROWS, D), F32), sds((D, FF), F32), sds((D, FF), F32), sds((8, FF), F32), sds((8, D), F32)),
            in_specs=vmem_specs(17),
            out_specs=tuple(vmem_specs(7)),
            scratch_shapes=[pltpu.VMEM((3 * D, D), BF16), pltpu.VMEM((ROWS, D), BF16), pltpu.VMEM((D, ROWS), BF16), pltpu.VMEM((D, ROWS), BF16)],
            compiler_params=pltpu.CompilerParams(vmem_limit_bytes=VMEM_LIMIT),
            cost_estimate=pl.CostEstimate(flops=12_000_000_000, bytes_accessed=22_000_000, transcendentals=3_000_000),
            name='tokens_a',
        )(x, g, ln1_gain, ln1_bias, ln2_gain, ln2_bias, wt, b_qkv, w_dense, b_dense, w_in, b_in, w_out, b_out, cos_t, sin_a, sin_b)

        heads = lax.all_to_all(send, 'sp', 0, 0, tiled=True)
        block = pl.BlockSpec((SP, 1, NT, 256), lambda b: (0, b, 0, 0))
        back = pl.pallas_call(
            heads_body,
            grid=(NB,),
            out_shape=sds((SP, NB, NT, 256), BF16),
            in_specs=[block],
            out_specs=block,
            scratch_shapes=[pltpu.VMEM((256, SEQ), BF16), pltpu.VMEM((SEQ, NT), F32), pltpu.VMEM((SEQ, NT), F32), pltpu.VMEM((SEQ, 128), F32)],
            compiler_params=pltpu.CompilerParams(vmem_limit_bytes=40 * 1024 * 1024),
            cost_estimate=pl.CostEstimate(flops=40_000_000_000, bytes_accessed=6_400_000, transcendentals=7_000_000),
            name='heads',
        )(heads)
        tok = lax.all_to_all(back, 'sp', 0, 0, tiled=True)

        g_wot = lax.psum_scatter(gwot.reshape(D, FF // 128, 128).transpose(1, 0, 2), grad_axes, scatter_dimension=0, tiled=True)
        g_wi = lax.psum_scatter(gwi, grad_axes, scatter_dimension=0, tiled=True)

        out, gx, pack = pl.pallas_call(
            tokens_b,
            out_shape=(sds((ROWS, D), BF16), sds((ROWS, D), BF16), sds((16, 136, D), F32)),
            in_specs=vmem_specs(15),
            out_specs=tuple(vmem_specs(3)),
            scratch_shapes=[pltpu.VMEM((3 * D, D), BF16), pltpu.VMEM((ROWS, D), BF16), pltpu.VMEM((ROWS, 3 * D), BF16)],
            compiler_params=pltpu.CompilerParams(vmem_limit_bytes=VMEM_LIMIT),
            cost_estimate=pl.CostEstimate(flops=4_000_000_000, bytes_accessed=20_000_000, transcendentals=0),
            name='tokens_b',
        )(tok, x, g, res, dh2, gbi, small, ln1_gain, ln1_bias, ln2_gain, wt, w_dense, cos_t, sin_a, sin_b)

        mine = lax.psum_scatter(pack.reshape(16 * 136, D), grad_axes, scatter_dimension=0, tiled=True)
        qkv = jnp.concatenate([mine[0:32], mine[32:64], mine[64:96]], axis=1)
        g_qk = qkv[:, :2 * D].reshape(32, NH, 2, HD)
        g_v = qkv[:, 2 * D:].reshape(32, NH, 1, HD)
        g_w_qkv = jnp.concatenate([g_qk, g_v], axis=2)
        tail = mine[128:136]
        return (out.reshape(hidden.shape), gx.reshape(hidden.shape), tail[0, 0:32], tail[1, 0:32], tail[2, 0:32], tail[3, 0:32], g_w_qkv,
                tail[0, 256:352], mine[96:128], tail[4, 0:32], g_wi, tail[0, 128:256], g_wot[0].T, tail[4, 0:32])

    tok_spec = P('dp', 'sp', None)
    grad_spec = P(grad_axes)
    return jax.shard_map(device_step, mesh=mesh, in_specs=(tok_spec, tok_spec) + (P(),) * 12, out_specs=(tok_spec, tok_spec) + (grad_spec,) * 12, check_vma=False)
```

time: 781 us -> 363 us (0.46)
  matrix products: 388 us -> 0 us
  local copies, waits for them, and re-layouts: 110 us -> 11.5 us
  Pallas kernels: 0 us -> 66.2 us
  blocking collectives: 33.2 us -> 84 us
  waiting for transfers between devices: 138 us -> 185 us
  other arithmetic: 48.4 us -> 2.12 us
  starting transfers between devices: 35.1 us -> 0.12 us
    dot_general x32 -> x0, matrix products: 306 us -> none  [the longest x4 86.3 us: one_block(): jnp.einsum('bhqk,bqhe->bkhe', ds_bf, q_part, preferred_element_type=jnp.f...]
    reduce_scatter x4 -> x3, waiting for transfers between devices: 94.2 us -> 184 us  [the longest x1 66.2 us: device_step(): lax.psum_scatter(gwot.reshape(D, FF // 128, 128).transpose(1, 0, 2), grad...]
    all_to_all x0 -> x2, blocking collectives: none -> 84 us  [the longest x1 43.1 us: device_step(): heads = lax.all_to_all(send, 'sp', 0, 0, tiled=True)]
    sub x8 -> x0, matrix products: 82 us -> none  [one_block(): attn_prob = jax.nn.softmax(jnp.where(causal, scores, -1e+30), axis=-1)]
    pallas_call x0 -> x3, Pallas kernels: none -> 66.2 us  [the longest x1 32.1 us: device_step(): pl.pallas_call(heads_body, grid=(NB,), out_shape=sds((SP, NB, NT, 256), B...]
    unnamed x104 -> x3, local copies, waits for them, and re-layouts: 49 us -> 0.51 us
    all_to_all x8 -> x0, waiting for transfers between devices: 43.7 us -> none  [the longest x4 33.7 us: to_heads(): return lax.all_to_all(tensor, 'sp', 2, 1, tiled=True)]
    all_to_all x8 -> x0, starting transfers between devices: 35 us -> none  [the longest x4 18.1 us: to_heads(): return lax.all_to_all(tensor, 'sp', 2, 1, tiled=True)]
  transfers between devices with their start and end apart: 12 -> 3, of which waited for: 8 -> 3; matrix products, arithmetic and copies ran while one was open for 29% -> 3% of each run, Pallas kernels for 0% -> 0%
where the time goes in v1:
time: 363 us; the launch traced here: 362 us
  waiting for transfers between devices  185 us (51%)
  blocking collectives  84 us (23%)
  Pallas kernels  66.2 us (18%)
  between operations  13.8 us (4%)
  local copies, waits for them, and re-layouts  11.5 us (3%)
    reduce_scatter x1, waiting for transfers between devices, device_step(): lax.psum_scatter(gwot.reshape(D, FF // 128, 128).transpose(1, 0, 2), grad...  66.2 us
    reduce_scatter x1, waiting for transfers between devices, device_step(): g_wi = lax.psum_scatter(gwi, grad_axes, scatter_dimension=0, tiled=True)  59.8 us
    reduce_scatter x1, waiting for transfers between devices, device_step(): lax.psum_scatter(pack.reshape(16 * 136, D), grad_axes, scatter_dimension=...  57.9 us
    all_to_all x1, blocking collectives, device_step(): heads = lax.all_to_all(send, 'sp', 0, 0, tiled=True)  43.1 us
    all_to_all x1, blocking collectives, device_step(): tok = lax.all_to_all(back, 'sp', 0, 0, tiled=True)  40.9 us
    pallas_call x1, Pallas kernels, device_step(): pl.pallas_call(heads_body, grid=(NB,), out_shape=sds((SP, NB, NT, 256), B...  32.1 us
    pallas_call x1, Pallas kernels, device_step(): pl.pallas_call(tokens_a, out_shape=(sds((SP, NB, NT, 256), BF16), sds((RO...  21.4 us
    pallas_call x1, Pallas kernels, device_step(): pl.pallas_call(tokens_b, out_shape=(sds((ROWS, D), BF16), sds((ROWS, D),...  12.7 us
  transfers between devices with their start and end apart: 3, of which 3 were waited for; matrix products, arithmetic and copies ran while one was open for 3% of the time, Pallas kernels for 0%

profile of v1, /device:TPU:0, one launch (start us, length us, event | category | flops | bytes accessed | tf_op | source)
XLA Modules:
  0.0 362.3 jit_solution(14676286391042341408)
XLA Ops:
  7.2 0.0 reduce-scatter.4.cloned.1.call-start
  7.3 1.3 fusion
  8.6 21.4 %tokens_a.1 = (bf16[8,3,256,256]{3,2,1,0:T(8,128)(2,1)}, f32[768,512]{1,0:T(8,128)}, f32[768,512]{1,0:T(8,128)}, f32[512,2048]{1,0:T(8,128)}, f32[512,2048]{1,0:...) custom-call(bf16[768,512]{1,0:T(8,128)(2,1)} %bitcast.34, bf16[768,512]{1,0:T(8,128)(2,1)} %bitcast.36, f32[512]{0:T(512)} %g1_ref.3, ...), custom_call_target="tpu_custom_call" | custom-call | flops 12000000000 | bytes 22000000 | tf_op jit(solution)/shard_map/tokens_a/pallas_call | solution.py:265
  30.0 43.1 %all_to_all.10.in_ref = bf16[8,3,256,256]{3,2,1,0:T(8,128)(2,1)S(1)} all-to-all(bf16[8,3,256,256]{3,2,1,0:T(8,128)(2,1)} %get-tuple-element.24), channel_id=1, replica_groups=mesh['dp'=2,'sp'=8] {'sp'}, dimensions={0} | all-to-all | bytes 6291456 | tf_op jit(solution)/shard_map/all_to_all | solution.py:276
  73.0 32.1 %heads.1 = bf16[8,3,256,256]{3,2,1,0:T(8,128)(2,1)S(1)} custom-call(bf16[8,3,256,256]{3,2,1,0:T(8,128)(2,1)S(1)} %all_to_all.10.in_ref), custom_call_target="tpu_custom_call" | custom-call | flops 40000000000 | bytes 6400000 | tf_op jit(solution)/shard_map/heads/pallas_call | solution.py:278
  105.1 40.9 %all_to_all.11.z_ref = bf16[8,3,256,256]{3,2,1,0:T(8,128)(2,1)} all-to-all(bf16[8,3,256,256]{3,2,1,0:T(8,128)(2,1)S(1)} %heads.1), channel_id=1, replica_groups=mesh['dp'=2,'sp'=8] {'sp'}, dimensions={0} | all-to-all | bytes 6291456 | tf_op jit(solution)/shard_map/all_to_all | solution.py:289
  146.1 12.7 %tokens_b.1 = (bf16[768,512]{1,0:T(8,128)(2,1)}, bf16[768,512]{1,0:T(8,128)(2,1)}, f32[16,136,512]{2,1,0:T(8,128)}) custom-call(bf16[8,3,256,256]{3,2,1,0:T(8,128)(2,1)} %all_to_all.11.z_ref, bf16[768,512]{1,0:T(8,128)(2,1)} %bitcast.35, bf16[768,512]{1,0:T(8,128)(2,1)} %bitcast.37, f32[768,512]{1,0:T(8,128)} %get-tuple-element.25.res_ref, ...), custom_call_target="tpu_custom_call" | custom-call | flops 4000000000 | bytes 20000000 | tf_op jit(solution)/shard_map/tokens_b/pallas_call | solution.py:294
  158.8 0.0 reduce-scatter.4.cloned.1.call-update
  158.8 0.0 reduce-scatter.6.cloned.1.call-start
  158.9 0.7 reduce-scatter.6.cloned.1.call-update
  159.6 0.0 reduce-scatter.8.cloned.1.call-start
  159.6 5.3 %copy.31 = f32[512,2048]{0,1:T(8,128)} copy(f32[512,2048]{1,0:T(8,128)} %get-tuple-element.33) | data formatting | bytes 8388608 | tf_op jit(solution)/shard_map/reshape | solution.py:291
  165.0 0.0 reduce-scatter.8.cloned.1.call-update
  165.0 57.9 %reduce-scatter.4.cloned.1.call-done = f32[136,512]{1,0:T(8,128)} async-done(((f32[2176,512]{1,0:T(8,128)}), f32[136,512]{1,0:T(8,128)}) %reduce-scatter.4.cloned.1.call-update) | async-done | bytes 278544 | tf_op jit(solution)/shard_map/reduce_scatter | solution.py:305
  222.9 1.4 slice_bitcast_fusion.1
  224.3 0.0 copy-start
  224.3 1.6 fusion.10
  225.8 0.1 reshape.106
  226.0 0.2 reshape.105
  226.2 0.8 pad_maximum_fusion
  227.0 1.2 slice_bitcast_fusion
  228.1 1.2 slice_bitcast_fusion.2
  229.3 59.8 %reduce-scatter.6.cloned.1.call-done = f32[32,2048]{1,0:T(8,128)} async-done(((f32[512,2048]{1,0:T(8,128)}), f32[32,2048]{1,0:T(8,128)}) %reduce-scatter.6.cloned.1.call-update) | async-done | bytes 262160 | tf_op jit(solution)/shard_map/reduce_scatter | solution.py:292
  289.1 66.2 %reduce-scatter.8.cloned.1.call-done = f32[1,512,128]{1,2,0:T(8,128)} async-done(((f32[16,512,128]{1,2,0:T(8,128)}), f32[1,512,128]{1,2,0:T(8,128)}) %reduce-scatter.8.cloned.1.call-update) | async-done | bytes 262160 | tf_op jit(solution)/shard_map/reduce_scatter | solution.py:291
  355.2 0.5 copy.33
  355.8 0.0 copy-done
  (6 shorter events, 0.1 us)
Async XLA Ops:
  7.2 215.7 %reduce-scatter.4.cloned.1.call-start = ((), (), s32[]{:S(2)}) async-start(), calls=%async_computation.5 | async-start | bytes 4734976 | tf_op jit(solution)/shard_map/reduce_scatter | solution.py:305
  158.8 130.3 %reduce-scatter.6.cloned.1.call-start = ((), (), s32[]{:S(2)}) async-start(), calls=%async_computation.6 | async-start | bytes 4456448 | tf_op jit(solution)/shard_map/reduce_scatter | solution.py:292
  159.6 195.7 %reduce-scatter.8.cloned.1.call-start = ((), (), s32[]{:S(2)}) async-start(), calls=%async_computation.7 | async-start | bytes 4456448 | tf_op jit(solution)/shard_map/reduce_scatter | solution.py:291
  224.3 131.5 %copy-start = (f32[32]{0:T(128)}, f32[32]{0:T(128)S(1)}, u32[]{:S(2)}) copy-start(f32[32]{0:T(128)S(1)} %get-tuple-element.75) | copy-start | bytes 388
Sparse Core Ops, SparseCore 0:
  158.9 63.8 reduce-scatter.3
  225.7 63.3 reduce-scatter.5
  291.9 63.2 reduce-scatter.7

commit v2 on v1

v2 whole, which is shorter than its diff:
```python
import math
import jax
import jax.numpy as jnp
from jax import lax
from jax.experimental import pallas as pl
from jax.experimental.pallas import tpu as pltpu
from jax.sharding import PartitionSpec as P

LN_EPS = 1e-5
ROPE_BASE = 10000.0
F32 = jnp.float32
BF16 = jnp.bfloat16
VMEM_LIMIT = 67_043_328
MESH = pl.DeviceIdType.MESH

NB, NT, D, NH, HD, FF = 3, 256, 512, 8, 64, 2048
ROWS = NB * NT
SP = 8
SEQ = SP * NT
CHUNK = 512


def dot(a, b):
    return lax.dot_general(a, b, (((1,), (0,)), ((), ())), preferred_element_type=F32)


def dot_tb(a, b):
    return lax.dot_general(a, b, (((1,), (1,)), ((), ())), preferred_element_type=F32)


def lane_iota(rows, cols):
    return lax.broadcasted_iota(jnp.int32, (rows, cols), 1)


def row(ref):
    return ref[...].reshape(1, ref.shape[0])


def layer_hat(x):
    mean_val = jnp.mean(x, axis=-1, keepdims=True)
    centered = x - mean_val
    var_val = jnp.mean(centered * centered, axis=-1, keepdims=True)
    inv_std = lax.rsqrt(var_val + LN_EPS)
    return centered * inv_std, inv_std


def fold_weights(wt_ref, wp_ref):
    for h in range(NH):
        wp_ref[2 * HD * h:2 * HD * (h + 1), :] = wt_ref[3 * HD * h:3 * HD * h + 2 * HD, :]
        wp_ref[2 * D + HD * h:2 * D + HD * (h + 1), :] = wt_ref[3 * HD * h + 2 * HD:3 * HD * (h + 1), :]


def pair_lanes(row_qk, row_v):
    low = lane_iota(row_qk.shape[0], 128) < HD
    tiles = []
    for p in range(NH // 2):
        first = row_qk[:, 256 * p:256 * p + 128]
        second = pltpu.roll(row_qk[:, 256 * p + 128:256 * p + 256], HD, 1)
        v_pair = row_v[:, 128 * p:128 * p + 128]
        tiles += [first, jnp.where(low, v_pair, second), jnp.where(low, second, v_pair)]
    return jnp.concatenate(tiles, axis=1)


def part_bits(p):
    return p % 2, p // 8, (p // 2) % 2, (p // 4) % 2


class Where:
    def __init__(self):
        self.z = lax.axis_index('dp')
        self.me = lax.axis_index('sp')
        self.bit = {'c': self.me % 2, 'x': (self.me // 2) % 2, 'y': self.me // 4, 'z': self.z}

    def flip(self, names):
        step = {'c': 1, 'x': 2, 'y': 4}
        sp = self.me
        z = self.z
        for n in names:
            if n == 'z':
                z = 1 - z
            else:
                sp = sp + step[n] * (1 - 2 * self.bit[n])
        return z, sp


class Summed:
    def __init__(self, at, order, buf, lands, send_sem, recv_sem):
        self.at, self.order, self.buf, self.lands, self.send_sem, self.recv_sem = at, order, buf, lands, send_sem, recv_sem

    def copy(self, k):
        mine = [self.at.bit[n] for n in self.order]
        index = tuple(mine[:k]) + (1 - mine[k],)
        z, sp = self.at.flip(self.order[k])
        return pltpu.make_async_remote_copy(src_ref=self.buf.at[index], dst_ref=self.lands[k], send_sem=self.send_sem.at[k], recv_sem=self.recv_sem.at[k],
                                            device_id=(z, sp), device_id_type=MESH)

    def start(self, k):
        self.copy(k).start()

    def land(self, k):
        self.copy(k).wait_recv()
        mine = tuple(self.at.bit[n] for n in self.order[:k + 1])
        rest = 3 - k
        for n in range(2 ** rest):
            sub = tuple((n >> (rest - 1 - m)) % 2 for m in range(rest))
            full = mine + sub
            self.buf[full] = self.buf[full] + self.lands[k][sub if sub else ...]

    def result(self):
        return self.buf[tuple(self.at.bit[n] for n in self.order)]

    def drain(self):
        for k in range(4):
            self.copy(k).wait_send()


PEERS = ('x', 'y', 'xy', 'xc', 'yc', 'xyc', 'c')


def exchange(at, b, src, dst, send_sem, recv_sem):
    out = []
    for k, names in enumerate(PEERS):
        z, sp = at.flip(names)
        out.append(pltpu.make_async_remote_copy(src_ref=src.at[b, sp], dst_ref=dst.at[b, at.me], send_sem=send_sem.at[b, k], recv_sem=recv_sem.at[b, k],
                                                device_id=(z, sp), device_id_type=MESH))
    return out


def layer(x_ref, g_ref, g1_ref, s1_ref, g2_ref, s2_ref, wt_ref, bqkv_ref, wd_ref, bd_ref, wi_ref, bi_ref, wo_ref, bo_ref, cos_ref, sa_ref, sb_ref,
          out_ref, gx_ref, gwi_ref, gwo_ref, gqkv_ref, gwd_ref, tail_ref,
          wp_ref, ctx_ref, dqkv_ref, h2t_ref, gt_ref, buf_ref, in_ref, z_ref, res_ref, dh2_ref, gbi_ref,
          xt_ref, sdp_ref, acc_ref,
          wi_buf, wi_c, wi_1, wi_2, wi_3, wo_buf, wo_c, wo_1, wo_2, wo_3,
          t0_buf, t0_c, t0_1, t0_2, t0_3, t1_buf, t1_c, t1_1, t1_2, t1_3, t2_buf, t2_c, t2_1, t2_2, t2_3,
          s1_sem, r1_sem, s2_sem, r2_sem, sum_send, sum_recv):
    at = Where()
    me = at.me
    sum_wi = Summed(at, 'czxy', wi_buf, (wi_c, wi_1, wi_2, wi_3), sum_send.at[0], sum_recv.at[0])
    sum_wo = Summed(at, 'czyx', wo_buf, (wo_c, wo_1, wo_2, wo_3), sum_send.at[1], sum_recv.at[1])
    sum_t = (Summed(at, 'czxy', t0_buf, (t0_c, t0_1, t0_2, t0_3), sum_send.at[2], sum_recv.at[2]),
             Summed(at, 'cxyz', t1_buf, (t1_c, t1_1, t1_2, t1_3), sum_send.at[3], sum_recv.at[3]),
             Summed(at, 'cyzx', t2_buf, (t2_c, t2_1, t2_2, t2_3), sum_send.at[4], sum_recv.at[4]))
    low = lane_iota(NT, 128) < HD
    fold_weights(wt_ref, wp_ref)
    b_all = row(bqkv_ref)

    for b in range(NB):
        rows = slice(NT * b, NT * (b + 1))
        x = x_ref[rows, :].astype(F32)
        hat, _ = layer_hat(x)
        h_b = (hat * row(g1_ref) + row(s1_ref)).astype(BF16)
        ctx_ref[rows, :] = (hat * row(g2_ref) + row(s2_ref)).astype(BF16)
        res_ref[rows, :] = x + row(bd_ref) + row(bo_ref)
        qk = dot_tb(h_b, wp_ref[:2 * D, :])
        vv = dot_tb(h_b, wp_ref[2 * D:, :])
        dc = dot_tb(g_ref[rows, :], wd_ref[...])
        for p in range(NH // 2):
            bias_a = b_all[:, 384 * p:384 * p + 128]
            bias_m = b_all[:, 384 * p + 128:384 * p + 256]
            bias_c = b_all[:, 384 * p + 256:384 * p + 384]
            low_row = low[:1]
            bias_b = pltpu.roll(jnp.where(low_row, bias_c, bias_m), HD, 1)
            bias_v = jnp.where(low_row, bias_m, bias_c)
            v_pair = vv[:, 128 * p:128 * p + 128] + bias_v
            d_pair = dc[:, 128 * p:128 * p + 128]
            v_turn = pltpu.roll(v_pair, HD, 1)
            d_turn = pltpu.roll(d_pair, HD, 1)
            for h, bias, second in ((2 * p, bias_a, jnp.where(low, v_pair, d_turn)), (2 * p + 1, bias_b, jnp.where(low, v_turn, d_pair))):
                t = qk[:, 128 * h:128 * h + 128] + bias
                t = t * cos_ref[...] + pltpu.roll(t, 120, 1) * sa_ref[...] + pltpu.roll(t, 8, 1) * sb_ref[...]
                buf_ref[b, h, :, 0:128] = t.astype(BF16)
                buf_ref[b, h, :, 128:256] = second.astype(BF16)
        if b == 0:
            barrier = pltpu.get_barrier_semaphore()
            for names in PEERS + ('z',):
                pl.semaphore_signal(barrier, inc=1, device_id=at.flip(names), device_id_type=MESH)
            pl.semaphore_wait(barrier, len(PEERS) + 1)
        for copy in exchange(at, b, buf_ref, in_ref, s1_sem, r1_sem):
            copy.start()
        in_ref[b, me] = buf_ref[b, me]

    h2t_ref[...] = ctx_ref[...].T
    gt_ref[...] = g_ref[...].T
    b_in = row(bi_ref)
    for c in range(FF // CHUNK):
        cols = slice(CHUNK * c, CHUNK * (c + 1))
        pre = dot(ctx_ref[...], wi_ref[:, cols]) + b_in[:, cols]
        d_act = dot_tb(g_ref[...], wo_ref[cols, :])
        cdf = 0.5 * (1.0 + lax.erf(pre * math.sqrt(0.5)))
        pdf = jnp.exp(-0.5 * pre * pre) * (1.0 / math.sqrt(2.0 * math.pi))
        act = (pre * cdf).astype(BF16)
        d_pre = d_act * (cdf + pre * pdf)
        d_pre_bf = d_pre.astype(BF16)
        gbi_ref[:, cols] = jnp.broadcast_to(jnp.sum(d_pre, axis=0, keepdims=True), (8, CHUNK))
        g_wo = dot(gt_ref[...], act)
        g_wi = dot(h2t_ref[...], d_pre_bf)
        for p in range(16):
            cc, zz, xx, yy = part_bits(p)
            wi_buf[cc, zz, xx, yy, 32 * c:32 * c + 32, :] = g_wi[32 * p:32 * p + 32]
        for q in range(4):
            cc, zz, xx, yy = part_bits(4 * c + q)
            for k in range(4):
                wo_buf[cc, zz, yy, xx, :, 128 * k:128 * k + 128] = g_wo[128 * k:128 * k + 128, 128 * q:128 * q + 128]
        res_ref[...] += dot(act, wo_ref[cols, :])
        d_h = dot_tb(d_pre_bf, wi_ref[:, cols])
        if c == 0:
            dh2_ref[...] = d_h
        else:
            dh2_ref[...] += d_h
    sum_wi.start(0)
    sum_wo.start(0)
    g_ln2 = jnp.zeros((1, D), F32)
    g_ln2_b = jnp.zeros((1, D), F32)
    g_b_dense = jnp.zeros((1, D), F32)
    for b in range(NB):
        rows = slice(NT * b, NT * (b + 1))
        hat, _ = layer_hat(x_ref[rows, :].astype(F32))
        d_h = dh2_ref[rows, :]
        g_ln2 += jnp.sum(d_h * hat, axis=0, keepdims=True)
        g_ln2_b += jnp.sum(d_h, axis=0, keepdims=True)
        g_b_dense += jnp.sum(g_ref[rows, :].astype(F32), axis=0, keepdims=True)
        dh2_ref[rows, :] = d_h * row(g2_ref)

    scale = 1.0 / math.sqrt(HD)
    keep = lax.broadcasted_iota(jnp.int32, (NT, NT), 0) <= lane_iota(NT, NT)
    zero_t = jnp.zeros((HD, NT), BF16)

    def one_sequence(b, carry):
        for copy in exchange(at, b, buf_ref, in_ref, s1_sem, r1_sem):
            copy.wait()
        for j in range(SP):
            xt_ref[:, NT * j:NT * (j + 1)] = in_ref[b, j].T
        for i in reversed(range(SP)):
            cols = slice(NT * i, NT * (i + 1))
            q_t = xt_ref[0:HD, cols] * BF16(scale)
            dc_t = xt_ref[3 * HD:4 * HD, cols]
            w_s = jnp.concatenate([zero_t, q_t, zero_t, zero_t], axis=0)
            w_p = jnp.concatenate([zero_t, zero_t, dc_t, zero_t], axis=0)
            w_sp = jnp.concatenate([w_s, w_p], axis=1)
            q_n = jnp.where(low, in_ref[b, i, :, 0:128] * BF16(scale), BF16(0.0))
            dc_n = jnp.where(low, BF16(0.0), in_ref[b, i, :, 128:256])
            w_acc = jnp.concatenate([q_n, dc_n], axis=0)
            top = None
            for j in range(i + 1):
                kv = slice(NT * j, NT * (j + 1))
                both = dot(in_ref[b, j], w_sp)
                s = both[:, :NT]
                if j == i:
                    s = jnp.where(keep, s, -1e30)
                sdp_ref[kv, 0:NT] = s
                sdp_ref[kv, NT:2 * NT] = both[:, NT:]
                part = jnp.max(s.reshape(NT // 8, 8, NT), axis=0)
                top = part if top is None else jnp.maximum(top, part)
            top = jnp.max(top, axis=0, keepdims=True)
            total = jnp.zeros((8, NT), F32)
            inner = jnp.zeros((8, NT), F32)
            for j in range(i + 1):
                kv = slice(NT * j, NT * (j + 1))
                e = jnp.exp(sdp_ref[kv, 0:NT] - top)
                sdp_ref[kv, 0:NT] = e
                total += jnp.sum(e.reshape(NT // 8, 8, NT), axis=0)
                inner += jnp.sum((e * sdp_ref[kv, NT:2 * NT]).reshape(NT // 8, 8, NT), axis=0)
            inv = 1.0 / jnp.sum(total, axis=0, keepdims=True)
            delta = jnp.sum(inner, axis=0, keepdims=True) * inv
            ctx_t = jnp.zeros((HD, NT), F32)
            dq_t = jnp.zeros((HD, NT), F32)
            for j in range(i + 1):
                kv = slice(NT * j, NT * (j + 1))
                prob = sdp_ref[kv, 0:NT] * inv
                prob_bf = prob.astype(BF16)
                ds_bf = (prob * (sdp_ref[kv, NT:2 * NT] - delta)).astype(BF16)
                ctx_t += dot(xt_ref[2 * HD:3 * HD, kv], prob_bf)
                dq_t += dot(xt_ref[HD:2 * HD, kv], ds_bf)
                step = dot(jnp.concatenate([ds_bf, prob_bf], axis=1), w_acc)
                if i == SP - 1:
                    acc_ref[kv, :] = step
                else:
                    acc_ref[kv, :] += step
            nat = jnp.concatenate([dq_t * scale, ctx_t], axis=0).T
            acc = acc_ref[cols, :]
            buf_ref[b, i, :, 0:128] = jnp.where(low, nat, pltpu.roll(acc, HD, 1)).astype(BF16)
            buf_ref[b, i, :, 128:256] = jnp.where(low, pltpu.roll(nat, HD, 1), acc).astype(BF16)
        for copy in exchange(at, b, buf_ref, z_ref, s2_sem, r2_sem):
            copy.start()
        z_ref[b, me] = buf_ref[b, me]

        @pl.when(b == 0)
        def _():
            for s in (sum_wi, sum_wo):
                s.land(0)
                s.start(1)
        return carry

    lax.fori_loop(0, NB, one_sequence, 0)

    g_ln1 = jnp.zeros((1, D), F32)
    g_ln1_b = jnp.zeros((1, D), F32)
    gb_qk = [None] * NH
    gb_v = [None] * (NH // 2)
    for b in range(NB):
        rows = slice(NT * b, NT * (b + 1))
        for copy in exchange(at, b, buf_ref, z_ref, s2_sem, r2_sem):
            copy.wait()
        for p in range(NH // 2):
            seconds = []
            for h in (2 * p, 2 * p + 1):
                t = z_ref[b, h, :, 0:128].astype(F32)
                t = t * cos_ref[...] - pltpu.roll(t, 120, 1) * sa_ref[...] - pltpu.roll(t, 8, 1) * sb_ref[...]
                part = jnp.sum(t, axis=0, keepdims=True)
                gb_qk[h] = part if b == 0 else gb_qk[h] + part
                dqkv_ref[rows, 128 * h:128 * h + 128] = t.astype(BF16)
                seconds.append(z_ref[b, h, :, 128:256].astype(F32))
            ctx_pair = jnp.where(low, seconds[0], pltpu.roll(seconds[1], HD, 1))
            dv_pair = jnp.where(low, pltpu.roll(seconds[0], HD, 1), seconds[1])
            ctx_ref[rows, 128 * p:128 * p + 128] = ctx_pair.astype(BF16)
            dqkv_ref[rows, 2 * D + 128 * p:2 * D + 128 * p + 128] = dv_pair.astype(BF16)
            part = jnp.sum(dv_pair, axis=0, keepdims=True)
            gb_v[p] = part if b == 0 else gb_v[p] + part
        out_ref[rows, :] = (res_ref[rows, :] + dot(ctx_ref[rows, :], wd_ref[...])).astype(BF16)
        hat, inv_std = layer_hat(x_ref[rows, :].astype(F32))
        h2t_ref[:, rows] = (hat * row(g1_ref) + row(s1_ref)).astype(BF16).T
        d_h1 = dot(dqkv_ref[rows, :], wp_ref[...])
        g_ln1 += jnp.sum(d_h1 * hat, axis=0, keepdims=True)
        g_ln1_b += jnp.sum(d_h1, axis=0, keepdims=True)
        d_hat = d_h1 * row(g1_ref) + dh2_ref[rows, :]
        d_x = inv_std * (d_hat - jnp.mean(d_hat, axis=-1, keepdims=True) - hat * jnp.mean(d_hat * hat, axis=-1, keepdims=True))
        gx_ref[rows, :] = (g_ref[rows, :].astype(F32) + d_x).astype(BF16)

    g_q = [dot(h2t_ref[...], dqkv_ref[:, D * k:D * (k + 1)]) for k in range(3)]
    g_dense = dot(ctx_ref[...].T, g_ref[...])
    five = jnp.concatenate([g_ln1, g_ln1_b, g_ln2, g_ln2_b, g_b_dense, jnp.zeros((3, D), F32)], axis=0)
    g_bqkv = jnp.broadcast_to(pair_lanes(jnp.concatenate(gb_qk, axis=1), jnp.concatenate(gb_v, axis=1)), (8, 3 * D))
    for p in range(16):
        cc, zz, xx, yy = part_bits(p)
        d0 = 32 * p
        t0_buf[cc, zz, xx, yy, 0:32, :] = g_q[0][d0:d0 + 32]
        t0_buf[cc, zz, xx, yy, 32:48, :] = g_q[1][d0:d0 + 16]
        t1_buf[cc, xx, yy, zz, 0:16, :] = g_q[1][d0 + 16:d0 + 32]
        t1_buf[cc, xx, yy, zz, 16:48, :] = g_q[2][d0:d0 + 32]
        t2_buf[cc, yy, zz, xx, 0:32, :] = g_dense[d0:d0 + 32]
        t2_buf[cc, yy, zz, xx, 32:40, 0:128] = pltpu.roll(five, (D - 32 * p) % D, 1)[:, 0:128] if p else five[:, 0:128]
        t2_buf[cc, yy, zz, xx, 32:40, 128:256] = gbi_ref[:, 128 * p:128 * p + 128]
        t2_buf[cc, yy, zz, xx, 32:40, 256:384] = pltpu.roll(g_bqkv, (3 * D - 96 * p) % (3 * D), 1)[:, 0:128] if p else g_bqkv[:, 0:128]
        t2_buf[cc, yy, zz, xx, 32:40, 384:512] = jnp.zeros((8, 128), F32)

    for s in sum_t:
        s.start(0)
    for s in (sum_wi, sum_wo):
        s.land(1)
        s.start(2)
    for k in range(3):
        for s in sum_t:
            s.land(k)
            s.start(k + 1)
        if k == 0:
            for s in (sum_wi, sum_wo):
                s.land(2)
                s.start(3)
        if k == 1:
            for s in (sum_wi, sum_wo):
                s.land(3)
    g_wi = sum_wi.result()
    for c in range(FF // CHUNK):
        gwi_ref[:, CHUNK * c:CHUNK * (c + 1)] = g_wi[32 * c:32 * c + 32]
    g_wo = sum_wo.result()
    for k in range(4):
        gwo_ref[:, 128 * k:128 * k + 128] = g_wo[:, 128 * k:128 * k + 128].T
    for s in sum_t:
        s.land(3)
    first, second, third = (s.result() for s in sum_t)
    gqkv_ref[:, 0:D] = first[0:32]
    gqkv_ref[0:16, D:2 * D] = first[32:48]
    gqkv_ref[16:32, D:2 * D] = second[0:16]
    gqkv_ref[:, 2 * D:3 * D] = second[16:48]
    gwd_ref[...] = third[0:32]
    tail_ref[...] = third[32:40]
    for s in (sum_wi, sum_wo) + sum_t:
        s.drain()


def sds(shape, dtype):
    return jax.ShapeDtypeStruct(shape, dtype)


def halving(rows):
    return [pltpu.VMEM((2,) * n + (rows, D), F32) for n in (4, 3, 2, 1, 0)]


def solution(mesh):
    grad_axes = ('dp', 'sp')

    def device_step(hidden, grad_out, ln1_gain, ln1_bias, ln2_gain, ln2_bias, w_qkv, b_qkv, w_dense, b_dense, w_in, b_in, w_out, b_out):
        x = hidden.reshape(ROWS, D)
        g = grad_out.reshape(ROWS, D)
        wt = jnp.transpose(w_qkv, (1, 2, 3, 0)).reshape(3 * D, D)
        rot = HD // 4
        half = rot // 2
        lane = jnp.arange(128)
        in_head = lane % HD
        inv_freq = ROPE_BASE ** (-(2.0 * (in_head % half)).astype(F32) / rot)
        pos = (lax.axis_index('sp') * NT + jnp.arange(NT)).astype(F32)
        angles = pos[:, None] * inv_freq[None, :]
        cos_t = jnp.where(in_head[None, :] < rot, jnp.cos(angles), 1.0)
        sin_t = jnp.sin(angles)
        sin_a = jnp.where(in_head[None, :] < half, -sin_t, 0.0)
        sin_b = jnp.where((in_head[None, :] >= half) & (in_head[None, :] < rot), sin_t, 0.0)

        dma = pltpu.SemaphoreType.DMA
        out, gx, g_wi, g_wo, qkv, g_wd, tail = pl.pallas_call(
            layer,
            out_shape=(sds((ROWS, D), BF16), sds((ROWS, D), BF16), sds((32, FF), F32), sds((128, D), F32), sds((32, 3 * D), F32), sds((32, D), F32), sds((8, D), F32)),
            in_specs=[pl.BlockSpec(memory_space=pltpu.VMEM)] * 17,
            out_specs=(pl.BlockSpec(memory_space=pltpu.VMEM),) * 7,
            scratch_shapes=[
                pltpu.VMEM((3 * D, D), BF16), pltpu.VMEM((ROWS, D), BF16), pltpu.VMEM((ROWS, 3 * D), BF16), pltpu.VMEM((D, ROWS), BF16), pltpu.VMEM((D, ROWS), BF16),
                pltpu.VMEM((NB, SP, NT, 256), BF16), pltpu.VMEM((NB, SP, NT, 256), BF16), pltpu.VMEM((NB, SP, NT, 256), BF16),
                pltpu.VMEM((ROWS, D), F32), pltpu.VMEM((ROWS, D), F32), pltpu.VMEM((8, FF), F32),
                pltpu.VMEM((256, SEQ), BF16), pltpu.VMEM((SEQ, 2 * NT), F32), pltpu.VMEM((SEQ, 128), F32),
                *halving(128), *halving(128), *halving(48), *halving(48), *halving(40),
                dma((NB, 7)), dma((NB, 7)), dma((NB, 7)), dma((NB, 7)), dma((5, 4)), dma((5, 4)),
            ],
            compiler_params=pltpu.CompilerParams(vmem_limit_bytes=VMEM_LIMIT, collective_id=0, has_side_effects=True),
            cost_estimate=pl.CostEstimate(flops=56_000_000_000, bytes_accessed=12_000_000, transcendentals=10_000_000),
            name='layer',
        )(x, g, ln1_gain, ln1_bias, ln2_gain, ln2_bias, wt, b_qkv, w_dense, b_dense, w_in, b_in, w_out, b_out, cos_t, sin_a, sin_b)

        g_qk = qkv[:, :2 * D].reshape(32, NH, 2, HD)
        g_v = qkv[:, 2 * D:].reshape(32, NH, 1, HD)
        g_w_qkv = jnp.concatenate([g_qk, g_v], axis=2)
        return (out.reshape(hidden.shape), gx.reshape(hidden.shape), tail[0, 0:32], tail[1, 0:32], tail[2, 0:32], tail[3, 0:32], g_w_qkv,
                tail[0, 256:352], g_wd, tail[4, 0:32], g_wi, tail[0, 128:256], g_wo, tail[4, 0:32])

    tok_spec = P('dp', 'sp', None)
    grad_spec = P(grad_axes)
    return jax.shard_map(device_step, mesh=mesh, in_specs=(tok_spec, tok_spec) + (P(),) * 12, out_specs=(tok_spec, tok_spec) + (grad_spec,) * 12, check_vma=False)
```

time: 363 us -> 133 us (0.37)
  waiting for transfers between devices: 185 us -> 0 us
  blocking collectives: 84 us -> 0 us
  Pallas kernels: 66.2 us -> 120 us
  between operations: 13.8 us -> 0.74 us
    reduce_scatter x3 -> x0, waiting for transfers between devices: 184 us -> none  [the longest x1 66.2 us: device_step(): lax.psum_scatter(gwot.reshape(D, FF // 128, 128).transpose(1, 0, 2), grad...]
    all_to_all x2 -> x0, blocking collectives: 84 us -> none  [the longest x1 43.1 us: device_step(): heads = lax.all_to_all(send, 'sp', 0, 0, tiled=True)]
    pallas_call x3 -> x1, Pallas kernels: 66.2 us -> 120 us  [device_step(): pl.pallas_call(layer, out_shape=(sds((ROWS, D), BF16), sds((ROWS, D), BF1...]
    reshape x1 -> x0, local copies, waits for them, and re-layouts: 5.34 us -> none  [device_step(): gwot.reshape(D, FF // 128, 128).transpose(1, 0, 2)]
    unnamed x3 -> x18, local copies, waits for them, and re-layouts: 0.51 us -> 4.33 us
  transfers between devices with their start and end apart: 3 -> 0, of which waited for: 3 -> 0; matrix products, arithmetic and copies ran while one was open for 3% -> 0% of each run, Pallas kernels for 0% -> 0%
where the time goes in v2:
time: 133 us
  Pallas kernels  120 us (90%)
  local copies, waits for them, and re-layouts  10.2 us (8%)
  other arithmetic  2.1 us (2%)
    pallas_call x1, Pallas kernels, device_step(): pl.pallas_call(layer, out_shape=(sds((ROWS, D), BF16), sds((ROWS, D), BF1...  120 us
    unnamed x18, local copies, waits for them, and re-layouts  4.33 us

profile of v2, /device:TPU:0, one launch (start us, length us, event | category | flops | bytes accessed | tf_op | source)
XLA Modules:
  0.0 132.9 jit_solution(9160497746308604733)
XLA Ops:
  0.7 1.3 fusion
  2.0 119.8 %layer.1 = (bf16[768,512]{1,0:T(8,128)(2,1)}, bf16[768,512]{1,0:T(8,128)(2,1)}, f32[32,2048]{1,0:T(8,128)}, f32[128,512]{1,0:T(8,128)}, f32[32,1536]{1,0:T(8,128)}, /*index=5*/f32[32,512]{1,0:T(8,128)}, f32[8,512]{1,0:T(8,128)}) custom-call(bf16[768,512]{1,0:T(8,128)(2,1)} %bitcast.26, bf16[768,512]{1,0:T(8,128)(2,1)} %bitcast.27, f32[512]{0:T(512)} %g1_ref.1, ...), custom_call_target="tpu_custom_call" | custom-call | flops 56000000000 | bytes 12000000 | tf_op jit(solution)/shard_map/layer/pallas_call | solution.py:409
  121.8 0.0 copy-start.1
  121.8 0.0 copy-start
  121.8 1.3 slice_bitcast_fusion.2
  123.1 1.2 slice_bitcast_fusion
  124.3 1.4 %slice_bitcast_fusion.1 = (f32[32]{0:T(128)S(1)}, f32[32]{0:T(128)}, f32[32]{0:T(128)}, f32[32]{0:T(128)}, f32[32]{0:T(128)}) fusion(f32[8,512]{1,0:T(8,128)} %get-tuple-element.23), kind=kLoop, calls=%fused_computation.20 | loop fusion | bytes 1280 | tf_op jit(solution)/shard_map/squeeze | solution.py:431
  125.7 0.0 copy-start.5
  125.7 0.8 slice.33
  126.5 0.9 slice.32
  127.4 0.1 reshape.99
  127.5 0.2 reshape.98
  127.7 0.0 copy-start.4
  127.7 0.0 copy-start.3
  127.8 0.8 pad_maximum_fusion
  128.5 0.0 copy-start.2
  128.5 0.5 copy.36
  129.0 0.0 copy-done.1
  129.1 0.9 copy.37
  129.9 0.0 copy-done
  129.9 0.9 copy.38
  130.8 0.0 copy-done.5
  130.8 0.0 copy-done.4
  130.8 0.6 copy.39
  131.4 0.0 copy-done.3
  131.5 0.7 copy.40
  132.2 0.0 copy-done.2
  132.2 0.7 copy.41
  (5 shorter events, 0.0 us)
Async XLA Ops:
  121.8 7.3 %copy-start.1 = (bf16[768,512]{1,0:T(8,128)(2,1)S(1)}, bf16[768,512]{1,0:T(8,128)(2,1)}, u32[]{:S(2)}) copy-start(bf16[768,512]{1,0:T(8,128)(2,1)} %get-tuple-element.21) | copy-start | bytes 2359300
  121.8 8.1 %copy-start = (bf16[768,512]{1,0:T(8,128)(2,1)S(1)}, bf16[768,512]{1,0:T(8,128)(2,1)}, u32[]{:S(2)}) copy-start(bf16[768,512]{1,0:T(8,128)(2,1)} %get-tuple-element.22) | copy-start | bytes 2359300
  125.7 5.2 %copy-start.5 = (f32[32]{0:T(128)}, f32[32]{0:T(128)S(1)}, u32[]{:S(2)}) copy-start(f32[32]{0:T(128)S(1)} %get-tuple-element.89) | copy-start | bytes 388
  127.7 3.1 %copy-start.4 = (f32[32,512]{1,0:T(8,128)S(1)}, f32[32,512]{1,0:T(8,128)}, u32[]{:S(2)}) copy-start(f32[32,512]{1,0:T(8,128)} %get-tuple-element.88) | copy-start | bytes 196612
  127.7 3.7 %copy-start.3 = (f32[32,2048]{1,0:T(8,128)S(1)}, f32[32,2048]{1,0:T(8,128)}, u32[]{:S(2)}) copy-start(f32[32,2048]{1,0:T(8,128)} %get-tuple-element.90) | copy-start | bytes 786436
  128.5 3.6 %copy-start.2 = (f32[128,512]{1,0:T(8,128)S(1)}, f32[128,512]{1,0:T(8,128)}, u32[]{:S(2)}) copy-start(f32[128,512]{1,0:T(8,128)} %get-tuple-element.92) | copy-start | bytes 786436

commit v3 on v2

v3 whole, which is shorter than its diff:
```python
import math
import jax
import jax.numpy as jnp
from jax import lax
from jax.experimental import pallas as pl
from jax.experimental.pallas import tpu as pltpu
from jax.sharding import PartitionSpec as P

LN_EPS = 1e-5
ROPE_BASE = 10000.0
F32 = jnp.float32
BF16 = jnp.bfloat16
MESH = pl.DeviceIdType.MESH
VMEM_LIMIT = 67_043_328

NB, NT, D, NH, HD, FF = 3, 256, 512, 8, 64, 2048
ROWS = NB * NT
SP = 8
PARTS = 16
SEQ = SP * NT
CHUNK = 512
N_CHUNK = FF // CHUNK
SUB = 8
LANES = 2 * HD
PAIRS = NH // 2
SLICE = D // PARTS
HALF = SLICE // 2
QKV = 3 * D
ROT = HD // 4
TURN = ROT // 2
TURN_BACK = LANES - TURN
LO = slice(0, LANES)
HI = slice(LANES, 2 * LANES)
SCALE = 1.0 / math.sqrt(HD)


def dot(a, b):
    return lax.dot_general(a, b, (((1,), (0,)), ((), ())), preferred_element_type=F32)


def dot_tb(a, b):
    return lax.dot_general(a, b, (((1,), (1,)), ((), ())), preferred_element_type=F32)


def span(index, size):
    return slice(size * index, size * (index + 1))


def lane_iota(rows, cols):
    return lax.broadcasted_iota(jnp.int32, (rows, cols), 1)


def swap(x):
    return pltpu.roll(x, HD, 1)


def row(ref):
    return ref[...].reshape(1, ref.shape[0])


def col_sum(x):
    return jnp.sum(x, axis=0, keepdims=True)


def fold(x, op):
    return op(x.reshape(NT // SUB, SUB, NT), axis=0)


def layer_hat(x):
    mean_val = jnp.mean(x, axis=-1, keepdims=True)
    centered = x - mean_val
    var_val = jnp.mean(centered * centered, axis=-1, keepdims=True)
    inv_std = lax.rsqrt(var_val + LN_EPS)
    return centered * inv_std, inv_std


def fold_weights(wt_ref, wp_ref):
    for h in range(NH):
        base = 3 * HD * h
        wp_ref[span(h, LANES), :] = wt_ref[base:base + LANES, :]
        wp_ref[span(2 * NH + h, HD), :] = wt_ref[base + LANES:base + LANES + HD, :]


def pair_lanes(row_qk, row_v):
    low = lane_iota(1, LANES) < HD
    tiles = []
    for p in range(PAIRS):
        second = swap(row_qk[:, span(2 * p + 1, LANES)])
        v_pair = row_v[:, span(p, LANES)]
        tiles += [row_qk[:, span(2 * p, LANES)], jnp.where(low, v_pair, second), jnp.where(low, second, v_pair)]
    return jnp.concatenate(tiles, axis=1)


def pair_bias(b_all, p):
    low = lane_iota(1, LANES) < HD
    first, mid, last = (b_all[:, span(3 * p + n, LANES)] for n in range(3))
    return first, swap(jnp.where(low, last, mid)), jnp.where(low, mid, last)


def cut(x, shift):
    width = x.shape[1]
    return pltpu.roll(x, (width - shift) % width, 1)[:, LO]


def part_bits(p):
    return {'c': p % 2, 'x': p // 2 % 2, 'y': p // 4 % 2, 'z': p // 8}


class Where:
    def __init__(self):
        self.z = lax.axis_index('dp')
        self.me = lax.axis_index('sp')
        self.bit = part_bits(self.z * SP + self.me)

    def flip(self, names):
        step = {'c': 1, 'x': 2, 'y': 4}
        z, sp = self.z, self.me
        for n in names:
            if n == 'z':
                z = 1 - z
            else:
                sp = sp + step[n] * (1 - 2 * self.bit[n])
        return z, sp


class Summed:
    def __init__(self, at, order, refs, send_sem, recv_sem):
        self.at, self.order, self.buf, self.lands, self.send_sem, self.recv_sem = at, order, refs[0], refs[1:], send_sem, recv_sem

    def place(self, p):
        bits = part_bits(p)
        return tuple(bits[n] for n in self.order)

    def put(self, p, rows, value):
        self.buf[self.place(p) + (rows,)] = value

    def copy(self, k):
        mine = [self.at.bit[n] for n in self.order]
        return pltpu.make_async_remote_copy(src_ref=self.buf.at[tuple(mine[:k]) + (1 - mine[k],)], dst_ref=self.lands[k],
                                            send_sem=self.send_sem.at[k], recv_sem=self.recv_sem.at[k],
                                            device_id=self.at.flip(self.order[k]), device_id_type=MESH)

    def start(self, k):
        self.copy(k).start()

    def land(self, k):
        self.copy(k).wait_recv()
        mine = tuple(self.at.bit[n] for n in self.order[:k + 1])
        rest = len(self.order) - 1 - k
        for n in range(2 ** rest):
            sub = tuple((n >> m) % 2 for m in reversed(range(rest)))
            self.buf[mine + sub] = self.buf[mine + sub] + self.lands[k][sub if sub else ...]

    def step(self, k):
        self.land(k)
        self.start(k + 1)

    def result(self):
        return self.buf[tuple(self.at.bit[n] for n in self.order)]

    def drain(self):
        for k in range(len(self.order)):
            self.copy(k).wait_send()


PEERS = ('x', 'y', 'xy', 'xc', 'yc', 'xyc', 'c')
ORDERS = ('czxy', 'czxy', 'czyx', 'czxy', 'cxyz', 'cyzx')
SUM_ROWS = (2 * SLICE, 2 * SLICE, LANES, SLICE + HALF, SLICE + HALF, SLICE + SUB)


def exchange(at, b, src, dst, sems):
    out = []
    for k, names in enumerate(PEERS):
        z, sp = at.flip(names)
        out.append(pltpu.make_async_remote_copy(src_ref=src.at[b, sp], dst_ref=dst.at[b, at.me], send_sem=sems[0].at[b, k], recv_sem=sems[1].at[b, k],
                                                device_id=(z, sp), device_id_type=MESH))
    return out


def layer(x_ref, g_ref, g1_ref, s1_ref, g2_ref, s2_ref, wt_ref, bqkv_ref, wd_ref, bd_ref, wi_hbm, bi_ref, wo_hbm, bo_ref, cos_ref, sa_ref, sb_ref,
          out_ref, gx_ref, gwi_ref, gwo_ref, gqkv_ref, gwd_ref, tail_ref,
          wi_ref, wo_ref, wp_ref, ctx_ref, dqkv_ref, h2t_ref, gt_ref, buf_ref, in_ref, z_ref, res_ref, dh2_ref, gbi_ref, xt_ref, sdp_ref, acc_ref,
          sums_refs, load_sem, out_sems, back_sems, sum_send, sum_recv):
    at = Where()
    me = at.me
    loads = [pltpu.make_async_copy(src, dst, load_sem.at[n]) for n, (src, dst) in enumerate(((wi_hbm, wi_ref), (wo_hbm, wo_ref)))]
    for load in loads:
        load.start()
    barrier = pltpu.get_barrier_semaphore()
    for names in PEERS + ('z',):
        pl.semaphore_signal(barrier, inc=1, device_id=at.flip(names), device_id_type=MESH)
    sums = [Summed(at, order, refs, sum_send.at[n], sum_recv.at[n]) for n, (order, refs) in enumerate(zip(ORDERS, sums_refs))]
    early, tail = sums[:3], sums[3:]
    sum_w = sums[:2]
    sum_wo = sums[2]
    low = lane_iota(NT, LANES) < HD
    fold_weights(wt_ref, wp_ref)
    b_all = row(bqkv_ref)

    for b in range(NB):
        rows = span(b, NT)
        x = x_ref[rows, :].astype(F32)
        hat, _ = layer_hat(x)
        h_b = (hat * row(g1_ref) + row(s1_ref)).astype(BF16)
        qk = dot_tb(h_b, wp_ref[:2 * D, :])
        vv = dot_tb(h_b, wp_ref[2 * D:, :])
        dc = dot_tb(g_ref[rows, :], wd_ref[...])
        for p in range(PAIRS):
            bias_a, bias_b, bias_v = pair_bias(b_all, p)
            v_pair = vv[:, span(p, LANES)] + bias_v
            d_pair = dc[:, span(p, LANES)]
            for h, bias, second in ((2 * p, bias_a, jnp.where(low, v_pair, swap(d_pair))), (2 * p + 1, bias_b, jnp.where(low, swap(v_pair), d_pair))):
                t = qk[:, span(h, LANES)] + bias
                t = t * cos_ref[...] + pltpu.roll(t, TURN_BACK, 1) * sa_ref[...] + pltpu.roll(t, TURN, 1) * sb_ref[...]
                buf_ref[b, h, :, LO] = t.astype(BF16)
                buf_ref[b, h, :, HI] = second.astype(BF16)
        if b == 0:
            pl.semaphore_wait(barrier, len(PEERS) + 1)
        for copy in exchange(at, b, buf_ref, in_ref, out_sems):
            copy.start()
        in_ref[b, me] = buf_ref[b, me]
        ctx_ref[rows, :] = (hat * row(g2_ref) + row(s2_ref)).astype(BF16)
        res_ref[rows, :] = x + row(bd_ref) + row(bo_ref)

    h2t_ref[...] = ctx_ref[...].T
    gt_ref[...] = g_ref[...].T
    b_in = row(bi_ref)
    for load in loads:
        load.wait()
    for c in range(N_CHUNK):
        cols = span(c, CHUNK)
        pre = dot(ctx_ref[...], wi_ref[:, cols]) + b_in[:, cols]
        d_act = dot_tb(g_ref[...], wo_ref[cols, :])
        cdf = 0.5 * (1.0 + lax.erf(pre * math.sqrt(0.5)))
        pdf = jnp.exp(-0.5 * pre * pre) * (1.0 / math.sqrt(2.0 * math.pi))
        act = (pre * cdf).astype(BF16)
        d_pre = d_act * (cdf + pre * pdf)
        d_pre_bf = d_pre.astype(BF16)
        gbi_ref[:, cols] = jnp.broadcast_to(col_sum(d_pre), (SUB, CHUNK))
        g_wi = dot(h2t_ref[...], d_pre_bf)
        for p in range(PARTS):
            sum_w[c // 2].put(p, span(c % 2, SLICE), g_wi[span(p, SLICE)])
        if c % 2:
            sum_w[c // 2].start(0)
        g_wo = dot(gt_ref[...], act)
        for q in range(CHUNK // LANES):
            where = sum_wo.place(PARTS // N_CHUNK * c + q)
            for k in range(D // LANES):
                sum_wo.buf[where + (slice(None), span(k, LANES))] = g_wo[span(k, LANES), span(q, LANES)]
        res_ref[...] += dot(act, wo_ref[cols, :])
        d_h = dot_tb(d_pre_bf, wi_ref[:, cols])
        if c == 0:
            dh2_ref[...] = d_h
        else:
            dh2_ref[...] += d_h
    sum_wo.start(0)
    sum_w[0].step(0)
    zero_row = jnp.zeros((1, D), F32)
    g_ln2 = g_ln2_b = g_b_dense = zero_row
    for b in range(NB):
        rows = span(b, NT)
        hat, _ = layer_hat(x_ref[rows, :].astype(F32))
        d_h = dh2_ref[rows, :]
        g_ln2 += col_sum(d_h * hat)
        g_ln2_b += col_sum(d_h)
        g_b_dense += col_sum(g_ref[rows, :].astype(F32))
        dh2_ref[rows, :] = d_h * row(g2_ref)

    keep = lax.broadcasted_iota(jnp.int32, (NT, NT), 0) <= lane_iota(NT, NT)
    zero_t = jnp.zeros((HD, NT), BF16)
    s_cols, p_cols = span(0, NT), span(1, NT)

    def one_sequence(b, carry):
        for copy in exchange(at, b, buf_ref, in_ref, out_sems):
            copy.wait()
        for j in range(SP):
            xt_ref[:, span(j, NT)] = in_ref[b, j].T
        for i in reversed(range(SP)):
            cols = span(i, NT)
            q_t = xt_ref[span(0, HD), cols] * BF16(SCALE)
            dc_t = xt_ref[span(3, HD), cols]
            w_s = jnp.concatenate([zero_t, q_t, zero_t, zero_t], axis=0)
            w_p = jnp.concatenate([zero_t, zero_t, dc_t, zero_t], axis=0)
            w_sp = jnp.concatenate([w_s, w_p], axis=1)
            q_n = jnp.where(low, in_ref[b, i, :, LO] * BF16(SCALE), BF16(0.0))
            dc_n = jnp.where(low, BF16(0.0), in_ref[b, i, :, HI])
            w_acc = jnp.concatenate([q_n, dc_n], axis=0)
            tops = []
            for j in range(i + 1):
                kv = span(j, NT)
                both = dot(in_ref[b, j], w_sp)
                s = both[:, s_cols]
                if j == i:
                    s = jnp.where(keep, s, -1e30)
                sdp_ref[kv, s_cols] = s
                sdp_ref[kv, p_cols] = both[:, p_cols]
                part = fold(s, jnp.max)
                tops = [jnp.maximum(tops[0], part)] if tops else [part]
            top = jnp.max(tops[0], axis=0, keepdims=True)
            total = jnp.zeros((SUB, NT), F32)
            inner = jnp.zeros((SUB, NT), F32)
            for j in range(i + 1):
                kv = span(j, NT)
                e = jnp.exp(sdp_ref[kv, s_cols] - top)
                sdp_ref[kv, s_cols] = e
                total += fold(e, jnp.sum)
                inner += fold(e * sdp_ref[kv, p_cols], jnp.sum)
            inv = 1.0 / col_sum(total)
            delta = col_sum(inner) * inv
            ctx_t = jnp.zeros((HD, NT), F32)
            dq_t = jnp.zeros((HD, NT), F32)
            for j in range(i + 1):
                kv = span(j, NT)
                prob = sdp_ref[kv, s_cols] * inv
                prob_bf = prob.astype(BF16)
                ds_bf = (prob * (sdp_ref[kv, p_cols] - delta)).astype(BF16)
                ctx_t += dot(xt_ref[span(2, HD), kv], prob_bf)
                dq_t += dot(xt_ref[span(1, HD), kv], ds_bf)
                step = dot(jnp.concatenate([ds_bf, prob_bf], axis=1), w_acc)
                if i == SP - 1:
                    acc_ref[kv, :] = step
                else:
                    acc_ref[kv, :] += step
            nat = jnp.concatenate([dq_t * SCALE, ctx_t], axis=0).T
            acc = acc_ref[cols, :]
            buf_ref[b, i, :, LO] = jnp.where(low, nat, swap(acc)).astype(BF16)
            buf_ref[b, i, :, HI] = jnp.where(low, swap(nat), acc).astype(BF16)
            if i == SP - 3:
                @pl.when(b == 0)
                def _():
                    for s in early[1:]:
                        s.step(0)
        for copy in exchange(at, b, buf_ref, z_ref, back_sems):
            copy.start()
        z_ref[b, me] = buf_ref[b, me]
        return carry

    lax.fori_loop(0, NB, one_sequence, 0)

    def arrive(b):
        rows = span(b, NT)
        for copy in exchange(at, b, buf_ref, z_ref, back_sems):
            copy.wait()
        if b == NB - 1:
            for s in early:
                s.step(1)
        sums_qk, sums_v = [], []
        for p in range(PAIRS):
            seconds = []
            for h in (2 * p, 2 * p + 1):
                t = z_ref[b, h, :, LO].astype(F32)
                t = t * cos_ref[...] - pltpu.roll(t, TURN_BACK, 1) * sa_ref[...] - pltpu.roll(t, TURN, 1) * sb_ref[...]
                sums_qk.append(col_sum(t))
                dqkv_ref[rows, span(h, LANES)] = t.astype(BF16)
                seconds.append(z_ref[b, h, :, HI].astype(F32))
            ctx_ref[rows, span(p, LANES)] = jnp.where(low, seconds[0], swap(seconds[1])).astype(BF16)
            dv_pair = jnp.where(low, swap(seconds[0]), seconds[1])
            dqkv_ref[rows, span(2 * NH // 2 + p, LANES)] = dv_pair.astype(BF16)
            sums_v.append(col_sum(dv_pair))
        hat, inv_std = layer_hat(x_ref[rows, :].astype(F32))
        h1_t = (hat * row(g1_ref) + row(s1_ref)).astype(BF16).T
        ctx_t = ctx_ref[rows, :].T
        for k in range(4):
            block = span(k, D)
            term = dot(h1_t, dqkv_ref[rows, block]) if k < 3 else dot(ctx_t, g_ref[rows, :])
            if b:
                sdp_ref[block, :] += term
            else:
                sdp_ref[block, :] = term
        return hat, inv_std, jnp.concatenate(sums_qk, axis=1), jnp.concatenate(sums_v, axis=1)

    def finish(b, hat, inv_std):
        rows = span(b, NT)
        d_h1 = dot(dqkv_ref[rows, :], wp_ref[...])
        d_hat = d_h1 * row(g1_ref) + dh2_ref[rows, :]
        d_x = inv_std * (d_hat - jnp.mean(d_hat, axis=-1, keepdims=True) - hat * jnp.mean(d_hat * hat, axis=-1, keepdims=True))
        gx_ref[rows, :] = (g_ref[rows, :].astype(F32) + d_x).astype(BF16)
        return col_sum(d_h1 * hat), col_sum(d_h1)

    def forward(b):
        rows = span(b, NT)
        out_ref[rows, :] = (res_ref[rows, :] + dot(ctx_ref[rows, :], wd_ref[...])).astype(BF16)

    g_ln1 = g_ln1_b = zero_row
    gb_qk, gb_v = jnp.zeros((1, 2 * D), F32), zero_row
    for b in range(NB):
        hat, inv_std, part_qk, part_v = arrive(b)
        gb_qk += part_qk
        gb_v += part_v
        if b == NB - 1:
            for p in range(PARTS):
                first = SLICE * p
                tail[0].put(p, span(0, SLICE), sdp_ref[first:first + SLICE, :])
                tail[0].put(p, slice(SLICE, SLICE + HALF), sdp_ref[D + first:D + first + HALF, :])
                tail[1].put(p, span(0, HALF), sdp_ref[D + first + HALF:D + first + SLICE, :])
                tail[1].put(p, slice(HALF, HALF + SLICE), sdp_ref[2 * D + first:2 * D + first + SLICE, :])
            for s in tail[:2]:
                s.start(0)
        part_g, part_b = finish(b, hat, inv_std)
        g_ln1 += part_g
        g_ln1_b += part_b
        if b < NB - 1:
            forward(b)

    five = jnp.concatenate([g_ln1, g_ln1_b, g_ln2, g_ln2_b, g_b_dense] + [zero_row] * 3, axis=0)
    g_bqkv = jnp.broadcast_to(pair_lanes(gb_qk, gb_v), (SUB, QKV))
    small = slice(SLICE, SLICE + SUB)
    for p in range(PARTS):
        tail[2].put(p, span(0, SLICE), sdp_ref[QKV + SLICE * p:QKV + SLICE * p + SLICE, :])
        line = [cut(five, SLICE * p), gbi_ref[:, span(p, LANES)], cut(g_bqkv, 3 * SLICE * p), jnp.zeros((SUB, LANES), F32)]
        tail[2].put(p, small, jnp.concatenate(line, axis=1))
    tail[2].start(0)
    forward(NB - 1)

    for s in tail:
        s.step(0)
    for s in early:
        s.step(2)
    for s in tail:
        s.step(1)
    for s in early:
        s.land(3)
    for c in range(N_CHUNK):
        gwi_ref[:, span(c, CHUNK)] = sum_w[c // 2].result()[span(c % 2, SLICE)]
    g_wo = sum_wo.result()
    for k in range(D // LANES):
        gwo_ref[:, span(k, LANES)] = g_wo[:, span(k, LANES)].T
    for s in tail:
        s.step(2)
    for s in tail:
        s.land(3)
    first, second, third = (s.result() for s in tail)
    gqkv_ref[:, span(0, D)] = first[:SLICE]
    gqkv_ref[:HALF, span(1, D)] = first[SLICE:]
    gqkv_ref[HALF:, span(1, D)] = second[:HALF]
    gqkv_ref[:, span(2, D)] = second[HALF:]
    gwd_ref[...] = third[:SLICE]
    tail_ref[...] = third[SLICE:]
    for s in sums:
        s.drain()


def write_out(out_in, gx_in, gwi_in, gwo_in, gqkv_in, gwd_in, tail_in,
              out_ref, gx_ref, g1_ref, s1_ref, g2_ref, s2_ref, gqkv_ref, gbqkv_ref, gwd_ref, gbd_ref, gwi_ref, gbi_ref, gwo_ref, gbo_ref):
    out_ref[...] = out_in[...]
    gx_ref[...] = gx_in[...]
    gwi_ref[...] = gwi_in[...]
    gwo_ref[...] = gwo_in[...]
    gwd_ref[...] = gwd_in[...]
    for h in range(NH):
        tile = gqkv_in[:, span(h, LANES)]
        gqkv_ref[:, 0, h, :] = tile[:, :HD]
        gqkv_ref[:, 1, h, :] = tile[:, HD:]
        gqkv_ref[:, 2, h, :] = gqkv_in[:, span(2 * NH + h, HD)]
    for n, ref in enumerate((g1_ref, s1_ref, g2_ref, s2_ref, gbd_ref)):
        ref[...] = tail_in[n, :SLICE]
    gbo_ref[...] = tail_in[n, :SLICE]
    gbi_ref[...] = tail_in[0, span(1, LANES)]
    gbqkv_ref[...] = tail_in[0, 2 * LANES:2 * LANES + 3 * SLICE]


def sds(shape, dtype):
    return jax.ShapeDtypeStruct(shape, dtype)


def halving(rows):
    return tuple(pltpu.VMEM((2,) * n + (rows, D), F32) for n in reversed(range(5)))


def vmem(rows, cols, dtype):
    return pltpu.VMEM((rows, cols), dtype)


def solution(mesh):
    grad_axes = ('dp', 'sp')

    def device_step(hidden, grad_out, ln1_gain, ln1_bias, ln2_gain, ln2_bias, w_qkv, b_qkv, w_dense, b_dense, w_in, b_in, w_out, b_out):
        x = hidden.reshape(ROWS, D)
        g = grad_out.reshape(ROWS, D)
        wt = jnp.moveaxis(w_qkv, 0, -1).reshape(QKV, D)
        in_head = (jnp.arange(LANES) % HD)[None, :]
        inv_freq = ROPE_BASE ** (-(2.0 * (in_head % TURN)).astype(F32) / ROT)
        pos = (lax.axis_index('sp') * NT + jnp.arange(NT)).astype(F32)
        angles = pos[:, None] * inv_freq
        cos_t = jnp.where(in_head < ROT, jnp.cos(angles), 1.0)
        sin_t = jnp.sin(angles)
        sin_a = jnp.where(in_head < TURN, -sin_t, 0.0)
        sin_b = jnp.where((in_head >= TURN) & (in_head < ROT), sin_t, 0.0)

        dma = pltpu.SemaphoreType.DMA
        whole = pl.BlockSpec(memory_space=pltpu.VMEM)
        in_specs = [whole] * 17
        in_specs[10] = in_specs[12] = pl.BlockSpec(memory_space=pl.ANY)
        block = pltpu.VMEM((NB, SP, NT, 2 * LANES), BF16)
        peer_sems = (dma((NB, len(PEERS))),) * 2
        results = pl.pallas_call(
            layer,
            out_shape=(sds((ROWS, D), BF16), sds((ROWS, D), BF16), sds((SLICE, FF), F32), sds((LANES, D), F32), sds((SLICE, QKV), F32), sds((SLICE, D), F32), sds((SUB, D), F32)),
            in_specs=in_specs,
            out_specs=(whole,) * 7,
            scratch_shapes=[
                vmem(D, FF, BF16), vmem(FF, D, BF16), vmem(QKV, D, BF16), vmem(ROWS, D, BF16), vmem(ROWS, QKV, BF16), vmem(D, ROWS, BF16), vmem(D, ROWS, BF16),
                block, block, block, vmem(ROWS, D, F32), vmem(ROWS, D, F32), vmem(SUB, FF, F32),
                vmem(2 * LANES, SEQ, BF16), vmem(SEQ, 2 * NT, F32), vmem(SEQ, LANES, F32),
                tuple(halving(rows) for rows in SUM_ROWS),
                dma((2,)), peer_sems, peer_sems, dma((6, 4)), dma((6, 4)),
            ],
            compiler_params=pltpu.CompilerParams(vmem_limit_bytes=VMEM_LIMIT, collective_id=0, has_side_effects=True),
            cost_estimate=pl.CostEstimate(flops=56_000_000_000, bytes_accessed=12_000_000, transcendentals=10_000_000),
            name='layer',
        )(x, g, ln1_gain, ln1_bias, ln2_gain, ln2_bias, wt, b_qkv, w_dense, b_dense, w_in, b_in, w_out, b_out, cos_t, sin_a, sin_b)

        part = sds((SLICE,), F32)
        tokens = sds((ROWS, D), BF16)
        final = list(pl.pallas_call(
            write_out,
            out_shape=(tokens, tokens, part, part, part, part, sds((SLICE, 3, NH, HD), F32), sds((3 * SLICE,), F32), sds((SLICE, D), F32), part,
                       sds((SLICE, FF), F32), sds((LANES,), F32), sds((LANES, D), F32), part),
            in_specs=[whole] * 7,
            out_specs=(whole,) * 14,
            name='write_out',
        )(*results))
        final[0] = final[0].reshape(hidden.shape)
        final[1] = final[1].reshape(hidden.shape)
        final[6] = jnp.swapaxes(final[6], 1, 2)
        return tuple(final)

    tok_spec = P('dp', 'sp', None)
    grad_spec = P(grad_axes)
    return jax.shard_map(device_step, mesh=mesh, in_specs=(tok_spec, tok_spec) + (P(),) * 12, out_specs=(tok_spec, tok_spec) + (grad_spec,) * 12, check_vma=False)
```

time: 133 us -> 120 us (0.902)
  local copies, waits for them, and re-layouts: 10.2 us -> 0 us
  Pallas kernels: 120 us -> 118 us
    pallas_call x1, Pallas kernels: 120 us -> 115 us  [device_step(): pl.pallas_call(layer, out_shape=(sds((ROWS, D), BF16), sds((ROWS, D), BF1...]
    unnamed x18 -> x0, local copies, waits for them, and re-layouts: 4.33 us -> none
    squeeze x3 -> x0, local copies, waits for them, and re-layouts: 3.86 us -> none  [the longest x1 1.38 us: device_step(): tail[4, 0:32]]
    pallas_call x0 -> x1, Pallas kernels: none -> 3.61 us  [device_step(): pl.pallas_call(write_out, out_shape=(tokens, tokens, part, part, part, pa...]
    slice x2 -> x0, local copies, waits for them, and re-layouts: 1.76 us -> none  [the longest x1 0.91 us: device_step(): g_qk = qkv[:, :2 * D].reshape(32, NH, 2, HD)]
where the time goes in v3:
time: 120 us
  Pallas kernels  118 us (98%)
  other arithmetic  1.33 us (1%)
    pallas_call x1, Pallas kernels, device_step(): pl.pallas_call(layer, out_shape=(sds((ROWS, D), BF16), sds((ROWS, D), BF1...  115 us
    pallas_call x1, Pallas kernels, device_step(): pl.pallas_call(write_out, out_shape=(tokens, tokens, part, part, part, pa...  3.61 us

profile of v3, /device:TPU:0, one launch (start us, length us, event | category | flops | bytes accessed | tf_op | source)
XLA Modules:
  0.0 120.3 jit_solution(1066061573135343603)
XLA Ops:
  0.7 1.3 %fusion = (f32[256,128]{1,0:T(8,128)}, f32[256,128]{1,0:T(8,128)}, f32[256,128]{1,0:T(8,128)}) fusion(f32[128]{0:T(128)S(1)} %fusion.8, f32[256]{0:T(256)S(1)} %add_convert_fusion, pred[128]{0:T(512)(128)(4,1)S(1)} %get-tuple-element.59, pred[128]{0:T(512)(128)(4,1)S(1)} %get-tuple-element.60, pred[128]{0:T(512)(128)(4,1)S(1)} %broadcast_compare_fusion.1), kind=kLoop, calls=%fused_computation.2 | loop fusion | flops 163840 | bytes 395136 | tf_op jit(solution)/shard_map/jit(_where)/select_n | solution.py:488
  2.0 114.6 %layer.1 = (bf16[768,512]{1,0:T(8,128)(2,1)}, bf16[768,512]{1,0:T(8,128)(2,1)}, f32[32,2048]{1,0:T(8,128)}, f32[128,512]{1,0:T(8,128)}, f32[32,1536]{1,0:T(8,128)}, /*index=5*/f32[32,512]{1,0:T(8,128)}, f32[8,512]{1,0:T(8,128)}) custom-call(bf16[768,512]{1,0:T(8,128)(2,1)} %bitcast.9, bf16[768,512]{1,0:T(8,128)(2,1)} %bitcast.10, f32[512]{0:T(512)} %g1_ref.1, ...), custom_call_target="tpu_custom_call" | custom-call | flops 56000000000 | bytes 12000000 | tf_op jit(solution)/shard_map/layer/pallas_call | solution.py:496
  116.6 3.6 %write_out.1 = (bf16[768,512]{1,0:T(8,128)(2,1)}, bf16[768,512]{1,0:T(8,128)(2,1)}, f32[32]{0:T(128)}, f32[32]{0:T(128)}, f32[32]{0:T(128)}, /*index=5*/f32[32]{...) custom-call(bf16[768,512]{1,0:T(8,128)(2,1)} %get-tuple-element.35.o, ...), custom_call_target="tpu_custom_call" | custom-call | tf_op jit(solution)/shard_map/write_out/pallas_call | solution.py:515
  (4 shorter events, 0.0 us)

commit v4 on v3

--- a/solution.py
+++ b/solution.py
@@ -1,6 +1,7 @@
 import math
 import jax
 import jax.numpy as jnp
+import numpy as np
 from jax import lax
 from jax.experimental import pallas as pl
 from jax.experimental.pallas import tpu as pltpu
@@ -21,10 +22,10 @@
 CHUNK = 512
 N_CHUNK = FF // CHUNK
 SUB = 8
+ROW_B_IN, ROW_B_QKV = 5, 6
 LANES = 2 * HD
 PAIRS = NH // 2
 SLICE = D // PARTS
-HALF = SLICE // 2
 QKV = 3 * D
 ROT = HD // 4
 TURN = ROT // 2
@@ -100,6 +101,23 @@
 def cut(x, shift):
     width = x.shape[1]
     return pltpu.roll(x, (width - shift) % width, 1)[:, LO]
+
+
+def rotation(near_ref, far_ref, block, cos_ref, sa_ref, sb_ref):
+    in_head = lane_iota(NT, LANES) % HD
+    near, far = near_ref[...], far_ref[pl.ds(block, 1), :]
+    near_s, far_s = pltpu.roll(near, LANES - ROT, 1), pltpu.roll(far, LANES - ROT, 1)
+    sin_t = near_s * far + near * far_s
+    cos_ref[...] = jnp.where(in_head < ROT, near * far - near_s * far_s, 1.0)
+    sa_ref[...] = jnp.where(in_head < TURN, -sin_t, 0.0)
+    sb_ref[...] = jnp.where((in_head >= TURN) & (in_head < ROT), sin_t, 0.0)
+
+
+def angle_table(positions):
+    lane = np.arange(LANES) % HD
+    freq = ROPE_BASE ** (-(2.0 * (lane % TURN)) / ROT)
+    angles = positions[:, None] * freq[None, :]
+    return np.where(lane < ROT, np.cos(angles), np.sin(angles)).astype(np.float32)
 
 
 def part_bits(p):
@@ -164,8 +182,8 @@
 
 
 PEERS = ('x', 'y', 'xy', 'xc', 'yc', 'xyc', 'c')
-ORDERS = ('czxy', 'czxy', 'czyx', 'czxy', 'cxyz', 'cyzx')
-SUM_ROWS = (2 * SLICE, 2 * SLICE, LANES, SLICE + HALF, SLICE + HALF, SLICE + SUB)
+ORDERS = ('czxy', 'czxy', 'czyx', 'czxy', 'czyx', 'cxzy', 'cyzx', 'czxy')
+SUM_SHAPES = ((2 * SLICE, D), (2 * SLICE, D), (LANES, D)) + ((SLICE, D),) * 4 + ((SUB, LANES),)
 
 
 def exchange(at, b, src, dst, sems):
@@ -177,10 +195,10 @@
     return out
 
 
-def layer(x_ref, g_ref, g1_ref, s1_ref, g2_ref, s2_ref, wt_ref, bqkv_ref, wd_ref, bd_ref, wi_hbm, bi_ref, wo_hbm, bo_ref, cos_ref, sa_ref, sb_ref,
-          out_ref, gx_ref, gwi_ref, gwo_ref, gqkv_ref, gwd_ref, tail_ref,
-          wi_ref, wo_ref, wp_ref, ctx_ref, dqkv_ref, h2t_ref, gt_ref, buf_ref, in_ref, z_ref, res_ref, dh2_ref, gbi_ref, xt_ref, sdp_ref, acc_ref,
-          sums_refs, load_sem, out_sems, back_sems, sum_send, sum_recv):
+def layer(x_ref, g_ref, g1_ref, s1_ref, g2_ref, s2_ref, wt_ref, bqkv_ref, wd_ref, bd_ref, wi_hbm, bi_ref, wo_hbm, bo_ref, near_ref, far_ref,
+          out_hbm, gx_hbm, gwi_ref, gwo_ref, gqkv_ref, gwd_ref, tail_ref,
+          out_ref, gx_ref, cos_ref, sa_ref, sb_ref, wi_ref, wo_ref, wp_ref, ctx_ref, dqkv_ref, h2t_ref, gt_ref, buf_ref, in_ref, z_ref, res_ref, dh2_ref, gbi_ref, xt_ref, sdp_ref, acc_ref,
+          sums_refs, load_sem, store_sem, out_sems, back_sems, sum_send, sum_recv):
     at = Where()
     me = at.me
     loads = [pltpu.make_async_copy(src, dst, load_sem.at[n]) for n, (src, dst) in enumerate(((wi_hbm, wi_ref), (wo_hbm, wo_ref)))]
@@ -194,6 +212,7 @@
     sum_w = sums[:2]
     sum_wo = sums[2]
     low = lane_iota(NT, LANES) < HD
+    rotation(near_ref, far_ref, me, cos_ref, sa_ref, sb_ref)
     fold_weights(wt_ref, wp_ref)
     b_all = row(bqkv_ref)
 
@@ -389,12 +408,9 @@
         gb_v += part_v
         if b == NB - 1:
             for p in range(PARTS):
-                first = SLICE * p
-                tail[0].put(p, span(0, SLICE), sdp_ref[first:first + SLICE, :])
-                tail[0].put(p, slice(SLICE, SLICE + HALF), sdp_ref[D + first:D + first + HALF, :])
-                tail[1].put(p, span(0, HALF), sdp_ref[D + first + HALF:D + first + SLICE, :])
-                tail[1].put(p, slice(HALF, HALF + SLICE), sdp_ref[2 * D + first:2 * D + first + SLICE, :])
-            for s in tail[:2]:
+                for k in range(3):
+                    tail[k].put(p, slice(None), sdp_ref[D * k + SLICE * p:D * k + SLICE * p + SLICE, :])
+            for s in tail[:3]:
                 s.start(0)
         part_g, part_b = finish(b, hat, inv_std)
         g_ln1 += part_g
@@ -402,15 +418,20 @@
         if b < NB - 1:
             forward(b)
 
+    store_gx = pltpu.make_async_copy(gx_ref, gx_hbm, store_sem.at[0])
+    store_gx.start()
     five = jnp.concatenate([g_ln1, g_ln1_b, g_ln2, g_ln2_b, g_b_dense] + [zero_row] * 3, axis=0)
     g_bqkv = jnp.broadcast_to(pair_lanes(gb_qk, gb_v), (SUB, QKV))
-    small = slice(SLICE, SLICE + SUB)
+    line = lax.broadcasted_iota(jnp.int32, (SUB, LANES), 0)
     for p in range(PARTS):
-        tail[2].put(p, span(0, SLICE), sdp_ref[QKV + SLICE * p:QKV + SLICE * p + SLICE, :])
-        line = [cut(five, SLICE * p), gbi_ref[:, span(p, LANES)], cut(g_bqkv, 3 * SLICE * p), jnp.zeros((SUB, LANES), F32)]
-        tail[2].put(p, small, jnp.concatenate(line, axis=1))
-    tail[2].start(0)
+        tail[3].put(p, slice(None), sdp_ref[QKV + SLICE * p:QKV + SLICE * p + SLICE, :])
+        small = jnp.where(line == ROW_B_IN, gbi_ref[:, span(p, LANES)], cut(five, SLICE * p))
+        tail[4].put(p, slice(None), jnp.where(line == ROW_B_QKV, cut(g_bqkv, 3 * SLICE * p), small))
+    for s in tail[3:]:
+        s.start(0)
     forward(NB - 1)
+    store_out = pltpu.make_async_copy(out_ref, out_hbm, store_sem.at[1])
+    store_out.start()
 
     for s in tail:
         s.step(0)
@@ -429,13 +450,12 @@
         s.step(2)
     for s in tail:
         s.land(3)
-    first, second, third = (s.result() for s in tail)
-    gqkv_ref[:, span(0, D)] = first[:SLICE]
-    gqkv_ref[:HALF, span(1, D)] = first[SLICE:]
-    gqkv_ref[HALF:, span(1, D)] = second[:HALF]
-    gqkv_ref[:, span(2, D)] = second[HALF:]
-    gwd_ref[...] = third[:SLICE]
-    tail_ref[...] = third[SLICE:]
+    for k in range(3):
+        gqkv_ref[:, span(k, D)] = tail[k].result()
+    gwd_ref[...] = tail[3].result()
+    tail_ref[...] = tail[4].result()
+    store_gx.wait()
+    store_out.wait()
     for s in sums:
         s.drain()
 
@@ -455,16 +475,16 @@
     for n, ref in enumerate((g1_ref, s1_ref, g2_ref, s2_ref, gbd_ref)):
         ref[...] = tail_in[n, :SLICE]
     gbo_ref[...] = tail_in[n, :SLICE]
-    gbi_ref[...] = tail_in[0, span(1, LANES)]
-    gbqkv_ref[...] = tail_in[0, 2 * LANES:2 * LANES + 3 * SLICE]
+    gbi_ref[...] = tail_in[ROW_B_IN, :]
+    gbqkv_ref[...] = tail_in[ROW_B_QKV, :3 * SLICE]
 
 
 def sds(shape, dtype):
     return jax.ShapeDtypeStruct(shape, dtype)
 
 
-def halving(rows):
-    return tuple(pltpu.VMEM((2,) * n + (rows, D), F32) for n in reversed(range(5)))
+def halving(shape):
+    return tuple(pltpu.VMEM((2,) * n + shape, F32) for n in reversed(range(5)))
 
 
 def vmem(rows, cols, dtype):
@@ -478,37 +498,30 @@
         x = hidden.reshape(ROWS, D)
         g = grad_out.reshape(ROWS, D)
         wt = jnp.moveaxis(w_qkv, 0, -1).reshape(QKV, D)
-        in_head = (jnp.arange(LANES) % HD)[None, :]
-        inv_freq = ROPE_BASE ** (-(2.0 * (in_head % TURN)).astype(F32) / ROT)
-        pos = (lax.axis_index('sp') * NT + jnp.arange(NT)).astype(F32)
-        angles = pos[:, None] * inv_freq
-        cos_t = jnp.where(in_head < ROT, jnp.cos(angles), 1.0)
-        sin_t = jnp.sin(angles)
-        sin_a = jnp.where(in_head < TURN, -sin_t, 0.0)
-        sin_b = jnp.where((in_head >= TURN) & (in_head < ROT), sin_t, 0.0)
-
+        near = jnp.asarray(angle_table(np.arange(NT)))
+        far = jnp.asarray(angle_table(NT * np.arange(SP)))
         dma = pltpu.SemaphoreType.DMA
         whole = pl.BlockSpec(memory_space=pltpu.VMEM)
-        in_specs = [whole] * 17
+        in_specs = [whole] * 16
         in_specs[10] = in_specs[12] = pl.BlockSpec(memory_space=pl.ANY)
         block = pltpu.VMEM((NB, SP, NT, 2 * LANES), BF16)
         peer_sems = (dma((NB, len(PEERS))),) * 2
         results = pl.pallas_call(
             layer,
-            out_shape=(sds((ROWS, D), BF16), sds((ROWS, D), BF16), sds((SLICE, FF), F32), sds((LANES, D), F32), sds((SLICE, QKV), F32), sds((SLICE, D), F32), sds((SUB, D), F32)),
+            out_shape=(sds((ROWS, D), BF16), sds((ROWS, D), BF16), sds((SLICE, FF), F32), sds((LANES, D), F32), sds((SLICE, QKV), F32), sds((SLICE, D), F32), sds((SUB, LANES), F32)),
             in_specs=in_specs,
-            out_specs=(whole,) * 7,
+            out_specs=(in_specs[10],) * 2 + (whole,) * 5,
             scratch_shapes=[
-                vmem(D, FF, BF16), vmem(FF, D, BF16), vmem(QKV, D, BF16), vmem(ROWS, D, BF16), vmem(ROWS, QKV, BF16), vmem(D, ROWS, BF16), vmem(D, ROWS, BF16),
+                vmem(ROWS, D, BF16), vmem(ROWS, D, BF16), vmem(NT, LANES, F32), vmem(NT, LANES, F32), vmem(NT, LANES, F32), vmem(D, FF, BF16), vmem(FF, D, BF16), vmem(QKV, D, BF16), vmem(ROWS, D, BF16), vmem(ROWS, QKV, BF16), vmem(D, ROWS, BF16), vmem(D, ROWS, BF16),
                 block, block, block, vmem(ROWS, D, F32), vmem(ROWS, D, F32), vmem(SUB, FF, F32),
                 vmem(2 * LANES, SEQ, BF16), vmem(SEQ, 2 * NT, F32), vmem(SEQ, LANES, F32),
-                tuple(halving(rows) for rows in SUM_ROWS),
-                dma((2,)), peer_sems, peer_sems, dma((6, 4)), dma((6, 4)),
+                tuple(halving(shape) for shape in SUM_SHAPES),
+                dma((2,)), dma((2,)), peer_sems, peer_sems, dma((8, 4)), dma((8, 4)),
             ],
             compiler_params=pltpu.CompilerParams(vmem_limit_bytes=VMEM_LIMIT, collective_id=0, has_side_effects=True),
             cost_estimate=pl.CostEstimate(flops=56_000_000_000, bytes_accessed=12_000_000, transcendentals=10_000_000),
             name='layer',
-        )(x, g, ln1_gain, ln1_bias, ln2_gain, ln2_bias, wt, b_qkv, w_dense, b_dense, w_in, b_in, w_out, b_out, cos_t, sin_a, sin_b)
+        )(x, g, ln1_gain, ln1_bias, ln2_gain, ln2_bias, wt, b_qkv, w_dense, b_dense, w_in, b_in, w_out, b_out, near, far)
 
         part = sds((SLICE,), F32)
         tokens = sds((ROWS, D), BF16)

time: 120 us -> 115 us (0.958)
  Pallas kernels: 118 us -> 114 us
  other arithmetic: 1.33 us -> 0 us
    pallas_call x1, Pallas kernels: 115 us -> 111 us  [device_step(): pl.pallas_call(layer, out_shape=(sds((ROWS, D), BF16), sds((ROWS, D), BF1...]
    select_n x1 -> x0, other arithmetic: 1.3 us -> none  [device_step(): sin_b = jnp.where((in_head >= TURN) & (in_head < ROT), sin_t, 0.0)]
where the time goes in v4:
time: 115 us
  Pallas kernels  114 us (99%)
    pallas_call x1, Pallas kernels, device_step(): pl.pallas_call(layer, out_shape=(sds((ROWS, D), BF16), sds((ROWS, D), BF1...  111 us
    pallas_call x1, Pallas kernels, device_step(): pl.pallas_call(write_out, out_shape=(tokens, tokens, part, part, part, pa...  3.59 us

profile of v4, /device:TPU:0, one launch (start us, length us, event | category | flops | bytes accessed | tf_op | source)
XLA Modules:
  0.0 115.1 jit_solution(9094836383585661791)
XLA Ops:
  0.7 110.8 %layer.1 = (bf16[768,512]{1,0:T(8,128)(2,1)}, bf16[768,512]{1,0:T(8,128)(2,1)}, f32[32,2048]{1,0:T(8,128)}, f32[128,512]{1,0:T(8,128)}, f32[32,1536]{1,0:T(8,128)}, /*index=5*/f32[32,512]{1,0:T(8,128)}, f32[8,128]{1,0:T(8,128)}) custom-call(bf16[768,512]{1,0:T(8,128)(2,1)} %bitcast.9, bf16[768,512]{1,0:T(8,128)(2,1)} %bitcast.10, f32[512]{0:T(512)} %g1_ref.1, ...), custom_call_target="tpu_custom_call" | custom-call | flops 56000000000 | bytes 12000000 | tf_op jit(solution)/shard_map/layer/pallas_call | solution.py:509
  111.4 3.6 %write_out.1 = (bf16[768,512]{1,0:T(8,128)(2,1)}, bf16[768,512]{1,0:T(8,128)(2,1)}, f32[32]{0:T(128)}, f32[32]{0:T(128)}, f32[32]{0:T(128)}, /*index=5*/f32[32]{...) custom-call(bf16[768,512]{1,0:T(8,128)(2,1)} %get-tuple-element.35.o, ...), custom_call_target="tpu_custom_call" | custom-call | tf_op jit(solution)/shard_map/write_out/pallas_call | solution.py:528

commit v5 on v4

--- a/solution.py
+++ b/solution.py
@@ -181,7 +181,7 @@
             self.copy(k).wait_send()
 
 
-PEERS = ('x', 'y', 'xy', 'xc', 'yc', 'xyc', 'c')
+PEERS = ('x', 'y', 'xc', 'yc', 'xy', 'xyc', 'c')
 ORDERS = ('czxy', 'czxy', 'czyx', 'czxy', 'czyx', 'cxzy', 'cyzx', 'czxy')
 SUM_SHAPES = ((2 * SLICE, D), (2 * SLICE, D), (LANES, D)) + ((SLICE, D),) * 4 + ((SUB, LANES),)
 
@@ -216,6 +216,10 @@
     fold_weights(wt_ref, wp_ref)
     b_all = row(bqkv_ref)
 
+    def send_heads(b):
+        for copy in exchange(at, b, buf_ref, in_ref, out_sems):
+            copy.start()
+
     for b in range(NB):
         rows = span(b, NT)
         x = x_ref[rows, :].astype(F32)
@@ -235,8 +239,7 @@
                 buf_ref[b, h, :, HI] = second.astype(BF16)
         if b == 0:
             pl.semaphore_wait(barrier, len(PEERS) + 1)
-        for copy in exchange(at, b, buf_ref, in_ref, out_sems):
-            copy.start()
+            send_heads(b)
         in_ref[b, me] = buf_ref[b, me]
         ctx_ref[rows, :] = (hat * row(g2_ref) + row(s2_ref)).astype(BF16)
         res_ref[rows, :] = x + row(bd_ref) + row(bo_ref)
@@ -268,6 +271,8 @@
                 sum_wo.buf[where + (slice(None), span(k, LANES))] = g_wo[span(k, LANES), span(q, LANES)]
         res_ref[...] += dot(act, wo_ref[cols, :])
         d_h = dot_tb(d_pre_bf, wi_ref[:, cols])
+        if c == N_CHUNK - 2:
+            send_heads(1)
         if c == 0:
             dh2_ref[...] = d_h
         else:
@@ -349,6 +354,7 @@
                 def _():
                     for s in early[1:]:
                         s.step(0)
+                    send_heads(2)
         for copy in exchange(at, b, buf_ref, z_ref, back_sems):
             copy.start()
         z_ref[b, me] = buf_ref[b, me]
@@ -358,11 +364,11 @@
 
     def arrive(b):
         rows = span(b, NT)
-        for copy in exchange(at, b, buf_ref, z_ref, back_sems):
-            copy.wait()
         if b == NB - 1:
             for s in early:
                 s.step(1)
+        for copy in exchange(at, b, buf_ref, z_ref, back_sems):
+            copy.wait()
         sums_qk, sums_v = [], []
         for p in range(PAIRS):
             seconds = []

time: 115 us -> 113 us (0.983)
  Pallas kernels: 114 us -> 112 us
    pallas_call x1, Pallas kernels: 111 us -> 108 us  [device_step(): pl.pallas_call(layer, out_shape=(sds((ROWS, D), BF16), sds((ROWS, D), BF1...]
where the time goes in v5:
time: 113 us
  Pallas kernels  112 us (99%)
    pallas_call x1, Pallas kernels, device_step(): pl.pallas_call(layer, out_shape=(sds((ROWS, D), BF16), sds((ROWS, D), BF1...  108 us
    pallas_call x1, Pallas kernels, device_step(): pl.pallas_call(write_out, out_shape=(tokens, tokens, part, part, part, pa...  3.59 us

profile of v5, /device:TPU:0, one launch (start us, length us, event | category | flops | bytes accessed | tf_op | source)
XLA Modules:
  0.0 112.5 jit_solution(2967674631198419212)
XLA Ops:
  0.7 108.2 %layer.1 = (bf16[768,512]{1,0:T(8,128)(2,1)}, bf16[768,512]{1,0:T(8,128)(2,1)}, f32[32,2048]{1,0:T(8,128)}, f32[128,512]{1,0:T(8,128)}, f32[32,1536]{1,0:T(8,128)}, /*index=5*/f32[32,512]{1,0:T(8,128)}, f32[8,128]{1,0:T(8,128)}) custom-call(bf16[768,512]{1,0:T(8,128)(2,1)} %bitcast.9, bf16[768,512]{1,0:T(8,128)(2,1)} %bitcast.10, f32[512]{0:T(512)} %g1_ref.1, ...), custom_call_target="tpu_custom_call" | custom-call | flops 56000000000 | bytes 12000000 | tf_op jit(solution)/shard_map/layer/pallas_call | solution.py:515
  108.8 3.6 %write_out.1 = (bf16[768,512]{1,0:T(8,128)(2,1)}, bf16[768,512]{1,0:T(8,128)(2,1)}, f32[32]{0:T(128)}, f32[32]{0:T(128)}, f32[32]{0:T(128)}, /*index=5*/f32[32]{...) custom-call(bf16[768,512]{1,0:T(8,128)(2,1)} %get-tuple-element.35.o, ...), custom_call_target="tpu_custom_call" | custom-call | tf_op jit(solution)/shard_map/write_out/pallas_call | solution.py:534

commit v6 on v5

--- a/solution.py
+++ b/solution.py
@@ -218,6 +218,10 @@
 
     def send_heads(b):
         for copy in exchange(at, b, buf_ref, in_ref, out_sems):
+            copy.start()
+
+    def send_tokens(b):
+        for copy in exchange(at, b, buf_ref, z_ref, back_sems):
             copy.start()
 
     for b in range(NB):
@@ -355,12 +359,15 @@
                     for s in early[1:]:
                         s.step(0)
                     send_heads(2)
-        for copy in exchange(at, b, buf_ref, z_ref, back_sems):
-            copy.start()
+
+                @pl.when(b > 0)
+                def _():
+                    send_tokens(b - 1)
         z_ref[b, me] = buf_ref[b, me]
         return carry
 
     lax.fori_loop(0, NB, one_sequence, 0)
+    send_tokens(NB - 1)
 
     def arrive(b):
         rows = span(b, NT)
@@ -388,10 +395,15 @@
         for k in range(4):
             block = span(k, D)
             term = dot(h1_t, dqkv_ref[rows, block]) if k < 3 else dot(ctx_t, g_ref[rows, :])
-            if b:
+            if b == 0:
+                sdp_ref[block, :] = term
+            elif b < NB - 1:
                 sdp_ref[block, :] += term
             else:
-                sdp_ref[block, :] = term
+                term = sdp_ref[block, :] + term
+                for p in range(PARTS):
+                    tail[k].put(p, slice(None), term[span(p, SLICE)])
+                tail[k].start(0)
         return hat, inv_std, jnp.concatenate(sums_qk, axis=1), jnp.concatenate(sums_v, axis=1)
 
     def finish(b, hat, inv_std):
@@ -413,11 +425,8 @@
         gb_qk += part_qk
         gb_v += part_v
         if b == NB - 1:
-            for p in range(PARTS):
-                for k in range(3):
-                    tail[k].put(p, slice(None), sdp_ref[D * k + SLICE * p:D * k + SLICE * p + SLICE, :])
-            for s in tail[:3]:
-                s.start(0)
+            for s in tail[:4]:
+                s.step(0)
         part_g, part_b = finish(b, hat, inv_std)
         g_ln1 += part_g
         g_ln1_b += part_b
@@ -430,17 +439,14 @@
     g_bqkv = jnp.broadcast_to(pair_lanes(gb_qk, gb_v), (SUB, QKV))
     line = lax.broadcasted_iota(jnp.int32, (SUB, LANES), 0)
     for p in range(PARTS):
-        tail[3].put(p, slice(None), sdp_ref[QKV + SLICE * p:QKV + SLICE * p + SLICE, :])
         small = jnp.where(line == ROW_B_IN, gbi_ref[:, span(p, LANES)], cut(five, SLICE * p))
         tail[4].put(p, slice(None), jnp.where(line == ROW_B_QKV, cut(g_bqkv, 3 * SLICE * p), small))
-    for s in tail[3:]:
-        s.start(0)
+    tail[4].start(0)
     forward(NB - 1)
     store_out = pltpu.make_async_copy(out_ref, out_hbm, store_sem.at[1])
     store_out.start()
 
-    for s in tail:
-        s.step(0)
+    tail[4].step(0)
     for s in early:
         s.step(2)
     for s in tail:
@@ -467,10 +473,15 @@
 
 
 def write_out(out_in, gx_in, gwi_in, gwo_in, gqkv_in, gwd_in, tail_in,
-              out_ref, gx_ref, g1_ref, s1_ref, g2_ref, s2_ref, gqkv_ref, gbqkv_ref, gwd_ref, gbd_ref, gwi_ref, gbi_ref, gwo_ref, gbo_ref):
-    out_ref[...] = out_in[...]
-    gx_ref[...] = gx_in[...]
+              out_ref, gx_ref, g1_ref, s1_ref, g2_ref, s2_ref, gqkv_ref, gbqkv_ref, gwd_ref, gbd_ref, gwi_ref, gbi_ref, gwo_ref, gbo_ref, out_buf, gx_buf, sems):
+    loads = [pltpu.make_async_copy(out_in, out_buf, sems.at[0]), pltpu.make_async_copy(gx_in, gx_buf, sems.at[1])]
+    stores = [pltpu.make_async_copy(out_buf, out_ref, sems.at[0]), pltpu.make_async_copy(gx_buf, gx_ref, sems.at[1])]
+    for load in loads:
+        load.start()
     gwi_ref[...] = gwi_in[...]
+    for load, store in zip(loads, stores):
+        load.wait()
+        store.start()
     gwo_ref[...] = gwo_in[...]
     gwd_ref[...] = gwd_in[...]
     for h in range(NH):
@@ -483,6 +494,8 @@
     gbo_ref[...] = tail_in[n, :SLICE]
     gbi_ref[...] = tail_in[ROW_B_IN, :]
     gbqkv_ref[...] = tail_in[ROW_B_QKV, :3 * SLICE]
+    for store in stores:
+        store.wait()
 
 
 def sds(shape, dtype):
@@ -535,8 +548,9 @@
             write_out,
             out_shape=(tokens, tokens, part, part, part, part, sds((SLICE, 3, NH, HD), F32), sds((3 * SLICE,), F32), sds((SLICE, D), F32), part,
                        sds((SLICE, FF), F32), sds((LANES,), F32), sds((LANES, D), F32), part),
-            in_specs=[whole] * 7,
-            out_specs=(whole,) * 14,
+            in_specs=[in_specs[10]] * 2 + [whole] * 5,
+            out_specs=(in_specs[10],) * 2 + (whole,) * 12,
+            scratch_shapes=[vmem(ROWS, D, BF16), vmem(ROWS, D, BF16), dma((2,))],
             name='write_out',
         )(*results))
         final[0] = final[0].reshape(hidden.shape)

time: 113 us -> 114 us (level)
  no operation moved by 1% of the time
where the time goes in v6:
time: 114 us
  Pallas kernels  113 us (99%)
    pallas_call x1, Pallas kernels, device_step(): pl.pallas_call(layer, out_shape=(sds((ROWS, D), BF16), sds((ROWS, D), BF1...  108 us
    pallas_call x1, Pallas kernels, device_step(): pl.pallas_call(write_out, out_shape=(tokens, tokens, part, part, part, pa...  4.4 us

profile of v6, /device:TPU:0, one launch (start us, length us, event | category | flops | bytes accessed | tf_op | source)
XLA Modules:
  0.0 113.6 jit_solution(4799905988876940150)
XLA Ops:
  0.7 108.4 %layer.1 = (bf16[768,512]{1,0:T(8,128)(2,1)}, bf16[768,512]{1,0:T(8,128)(2,1)}, f32[32,2048]{1,0:T(8,128)}, f32[128,512]{1,0:T(8,128)}, f32[32,1536]{1,0:T(8,128)}, /*index=5*/f32[32,512]{1,0:T(8,128)}, f32[8,128]{1,0:T(8,128)}) custom-call(bf16[768,512]{1,0:T(8,128)(2,1)} %bitcast.9, bf16[768,512]{1,0:T(8,128)(2,1)} %bitcast.10, f32[512]{0:T(512)} %g1_ref.1, ...), custom_call_target="tpu_custom_call" | custom-call | flops 56000000000 | bytes 12000000 | tf_op jit(solution)/shard_map/layer/pallas_call | solution.py:528
  109.0 4.4 %write_out.1 = (bf16[768,512]{1,0:T(8,128)(2,1)}, bf16[768,512]{1,0:T(8,128)(2,1)}, f32[32]{0:T(128)}, f32[32]{0:T(128)}, f32[32]{0:T(128)}, /*index=5*/f32[32]{...) custom-call(bf16[768,512]{1,0:T(8,128)(2,1)} %get-tuple-element.35.o, ...), custom_call_target="tpu_custom_call" | custom-call | tf_op jit(solution)/shard_map/write_out/pallas_call | solution.py:547

commit v7 on v6

--- a/solution.py
+++ b/solution.py
@@ -359,15 +359,11 @@
                     for s in early[1:]:
                         s.step(0)
                     send_heads(2)
-
-                @pl.when(b > 0)
-                def _():
-                    send_tokens(b - 1)
+        send_tokens(b)
         z_ref[b, me] = buf_ref[b, me]
         return carry
 
     lax.fori_loop(0, NB, one_sequence, 0)
-    send_tokens(NB - 1)
 
     def arrive(b):
         rows = span(b, NT)
@@ -447,10 +443,12 @@
     store_out.start()
 
     tail[4].step(0)
+    for s in tail:
+        s.step(1)
     for s in early:
         s.step(2)
     for s in tail:
-        s.step(1)
+        s.step(2)
     for s in early:
         s.land(3)
     for c in range(N_CHUNK):
@@ -458,8 +456,6 @@
     g_wo = sum_wo.result()
     for k in range(D // LANES):
         gwo_ref[:, span(k, LANES)] = g_wo[:, span(k, LANES)].T
-    for s in tail:
-        s.step(2)
     for s in tail:
         s.land(3)
     for k in range(3):
@@ -473,15 +469,10 @@
 
 
 def write_out(out_in, gx_in, gwi_in, gwo_in, gqkv_in, gwd_in, tail_in,
-              out_ref, gx_ref, g1_ref, s1_ref, g2_ref, s2_ref, gqkv_ref, gbqkv_ref, gwd_ref, gbd_ref, gwi_ref, gbi_ref, gwo_ref, gbo_ref, out_buf, gx_buf, sems):
-    loads = [pltpu.make_async_copy(out_in, out_buf, sems.at[0]), pltpu.make_async_copy(gx_in, gx_buf, sems.at[1])]
-    stores = [pltpu.make_async_copy(out_buf, out_ref, sems.at[0]), pltpu.make_async_copy(gx_buf, gx_ref, sems.at[1])]
-    for load in loads:
-        load.start()
+              out_ref, gx_ref, g1_ref, s1_ref, g2_ref, s2_ref, gqkv_ref, gbqkv_ref, gwd_ref, gbd_ref, gwi_ref, gbi_ref, gwo_ref, gbo_ref):
+    out_ref[...] = out_in[...]
+    gx_ref[...] = gx_in[...]
     gwi_ref[...] = gwi_in[...]
-    for load, store in zip(loads, stores):
-        load.wait()
-        store.start()
     gwo_ref[...] = gwo_in[...]
     gwd_ref[...] = gwd_in[...]
     for h in range(NH):
@@ -494,8 +485,6 @@
     gbo_ref[...] = tail_in[n, :SLICE]
     gbi_ref[...] = tail_in[ROW_B_IN, :]
     gbqkv_ref[...] = tail_in[ROW_B_QKV, :3 * SLICE]
-    for store in stores:
-        store.wait()
 
 
 def sds(shape, dtype):
@@ -548,9 +537,8 @@
             write_out,
             out_shape=(tokens, tokens, part, part, part, part, sds((SLICE, 3, NH, HD), F32), sds((3 * SLICE,), F32), sds((SLICE, D), F32), part,
                        sds((SLICE, FF), F32), sds((LANES,), F32), sds((LANES, D), F32), part),
-            in_specs=[in_specs[10]] * 2 + [whole] * 5,
-            out_specs=(in_specs[10],) * 2 + (whole,) * 12,
-            scratch_shapes=[vmem(ROWS, D, BF16), vmem(ROWS, D, BF16), dma((2,))],
+            in_specs=[whole] * 7,
+            out_specs=(whole,) * 14,
             name='write_out',
         )(*results))
         final[0] = final[0].reshape(hidden.shape)

time: 114 us -> 112 us (0.982)
  Pallas kernels: 113 us -> 111 us
    pallas_call x1, Pallas kernels: 108 us -> 107 us  [device_step(): pl.pallas_call(layer, out_shape=(sds((ROWS, D), BF16), sds((ROWS, D), BF1...]
where the time goes in v7:
time: 112 us
  Pallas kernels  111 us (99%)
    pallas_call x1, Pallas kernels, device_step(): pl.pallas_call(layer, out_shape=(sds((ROWS, D), BF16), sds((ROWS, D), BF1...  107 us
    pallas_call x1, Pallas kernels, device_step(): pl.pallas_call(write_out, out_shape=(tokens, tokens, part, part, part, pa...  3.59 us

profile of v7, /device:TPU:0, one launch (start us, length us, event | category | flops | bytes accessed | tf_op | source)
XLA Modules:
  0.0 111.5 jit_solution(15935517560027433935)
XLA Ops:
  0.7 107.2 %layer.1 = (bf16[768,512]{1,0:T(8,128)(2,1)}, bf16[768,512]{1,0:T(8,128)(2,1)}, f32[32,2048]{1,0:T(8,128)}, f32[128,512]{1,0:T(8,128)}, f32[32,1536]{1,0:T(8,128)}, /*index=5*/f32[32,512]{1,0:T(8,128)}, f32[8,128]{1,0:T(8,128)}) custom-call(bf16[768,512]{1,0:T(8,128)(2,1)} %bitcast.9, bf16[768,512]{1,0:T(8,128)(2,1)} %bitcast.10, f32[512]{0:T(512)} %g1_ref.1, ...), custom_call_target="tpu_custom_call" | custom-call | flops 56000000000 | bytes 12000000 | tf_op jit(solution)/shard_map/layer/pallas_call | solution.py:517
  107.8 3.6 %write_out.1 = (bf16[768,512]{1,0:T(8,128)(2,1)}, bf16[768,512]{1,0:T(8,128)(2,1)}, f32[32]{0:T(128)}, f32[32]{0:T(128)}, f32[32]{0:T(128)}, /*index=5*/f32[32]{...) custom-call(bf16[768,512]{1,0:T(8,128)(2,1)} %get-tuple-element.35.o, ...), custom_call_target="tpu_custom_call" | custom-call | tf_op jit(solution)/shard_map/write_out/pallas_call | solution.py:536

commit v8 on v7

--- a/solution.py
+++ b/solution.py
@@ -182,8 +182,8 @@
 
 
 PEERS = ('x', 'y', 'xc', 'yc', 'xy', 'xyc', 'c')
-ORDERS = ('czxy', 'czxy', 'czyx', 'czxy', 'czyx', 'cxzy', 'cyzx', 'czxy')
-SUM_SHAPES = ((2 * SLICE, D), (2 * SLICE, D), (LANES, D)) + ((SLICE, D),) * 4 + ((SUB, LANES),)
+ORDERS = ('czxy', 'czyx', 'czxy', 'czyx', 'czxy', 'czyx', 'cxzy', 'cyzx', 'czxy')
+SUM_SHAPES = ((HD, D),) * 4 + ((SLICE, D),) * 4 + ((SUB, LANES),)
 
 
 def exchange(at, b, src, dst, sems):
@@ -208,9 +208,8 @@
     for names in PEERS + ('z',):
         pl.semaphore_signal(barrier, inc=1, device_id=at.flip(names), device_id_type=MESH)
     sums = [Summed(at, order, refs, sum_send.at[n], sum_recv.at[n]) for n, (order, refs) in enumerate(zip(ORDERS, sums_refs))]
-    early, tail = sums[:3], sums[3:]
-    sum_w = sums[:2]
-    sum_wo = sums[2]
+    early, tail = sums[:4], sums[4:]
+    sum_w, sum_wo = sums[:2], sums[2:4]
     low = lane_iota(NT, LANES) < HD
     rotation(near_ref, far_ref, me, cos_ref, sa_ref, sb_ref)
     fold_weights(wt_ref, wp_ref)
@@ -270,9 +269,10 @@
             sum_w[c // 2].start(0)
         g_wo = dot(gt_ref[...], act)
         for q in range(CHUNK // LANES):
-            where = sum_wo.place(PARTS // N_CHUNK * c + q)
-            for k in range(D // LANES):
-                sum_wo.buf[where + (slice(None), span(k, LANES))] = g_wo[span(k, LANES), span(q, LANES)]
+            for n, s in enumerate(sum_wo):
+                where = s.place(PARTS // N_CHUNK * c + q)
+                for k in range(D // LANES):
+                    s.buf[where + (slice(None), span(k, LANES))] = g_wo[span(2 * k + n, HD), span(q, LANES)]
         res_ref[...] += dot(act, wo_ref[cols, :])
         d_h = dot_tb(d_pre_bf, wi_ref[:, cols])
         if c == N_CHUNK - 2:
@@ -281,7 +281,8 @@
             dh2_ref[...] = d_h
         else:
             dh2_ref[...] += d_h
-    sum_wo.start(0)
+    for s in sum_wo:
+        s.start(0)
     sum_w[0].step(0)
     zero_row = jnp.zeros((1, D), F32)
     g_ln2 = g_ln2_b = g_b_dense = zero_row
@@ -359,17 +360,23 @@
                     for s in early[1:]:
                         s.step(0)
                     send_heads(2)
+
+                @pl.when(b == 1)
+                def _():
+                    sum_w[0].step(1)
         send_tokens(b)
         z_ref[b, me] = buf_ref[b, me]
         return carry
 
     lax.fori_loop(0, NB, one_sequence, 0)
+    sum_w[0].step(2)
+    sum_w[1].step(1)
+    sum_wo[0].step(1)
 
     def arrive(b):
         rows = span(b, NT)
         if b == NB - 1:
-            for s in early:
-                s.step(1)
+            sum_wo[1].step(1)
         for copy in exchange(at, b, buf_ref, z_ref, back_sems):
             copy.wait()
         sums_qk, sums_v = [], []
@@ -445,7 +452,7 @@
     tail[4].step(0)
     for s in tail:
         s.step(1)
-    for s in early:
+    for s in early[1:]:
         s.step(2)
     for s in tail:
         s.step(2)
@@ -453,7 +460,7 @@
         s.land(3)
     for c in range(N_CHUNK):
         gwi_ref[:, span(c, CHUNK)] = sum_w[c // 2].result()[span(c % 2, SLICE)]
-    g_wo = sum_wo.result()
+    g_wo = jnp.concatenate([s.result() for s in sum_wo], axis=0)
     for k in range(D // LANES):
         gwo_ref[:, span(k, LANES)] = g_wo[:, span(k, LANES)].T
     for s in tail:
@@ -524,7 +531,7 @@
                 block, block, block, vmem(ROWS, D, F32), vmem(ROWS, D, F32), vmem(SUB, FF, F32),
                 vmem(2 * LANES, SEQ, BF16), vmem(SEQ, 2 * NT, F32), vmem(SEQ, LANES, F32),
                 tuple(halving(shape) for shape in SUM_SHAPES),
-                dma((2,)), dma((2,)), peer_sems, peer_sems, dma((8, 4)), dma((8, 4)),
+                dma((2,)), dma((2,)), peer_sems, peer_sems, dma((9, 4)), dma((9, 4)),
             ],
             compiler_params=pltpu.CompilerParams(vmem_limit_bytes=VMEM_LIMIT, collective_id=0, has_side_effects=True),
             cost_estimate=pl.CostEstimate(flops=56_000_000_000, bytes_accessed=12_000_000, transcendentals=10_000_000),

time: 112 us -> 115 us (1.027)
  Pallas kernels: 111 us -> 114 us
    pallas_call x1, Pallas kernels: 107 us -> 110 us  [device_step(): pl.pallas_call(layer, out_shape=(sds((ROWS, D), BF16), sds((ROWS, D), BF1...]
where the time goes in v8:
time: 115 us
  Pallas kernels  114 us (99%)
    pallas_call x1, Pallas kernels, device_step(): pl.pallas_call(layer, out_shape=(sds((ROWS, D), BF16), sds((ROWS, D), BF1...  110 us
    pallas_call x1, Pallas kernels, device_step(): pl.pallas_call(write_out, out_shape=(tokens, tokens, part, part, part, pa...  3.59 us

profile of v8, /device:TPU:0, one launch (start us, length us, event | category | flops | bytes accessed | tf_op | source)
XLA Modules:
  0.0 114.8 jit_solution(13070997823864859044)
XLA Ops:
  0.7 110.5 %layer.1 = (bf16[768,512]{1,0:T(8,128)(2,1)}, bf16[768,512]{1,0:T(8,128)(2,1)}, f32[32,2048]{1,0:T(8,128)}, f32[128,512]{1,0:T(8,128)}, f32[32,1536]{1,0:T(8,128)}, /*index=5*/f32[32,512]{1,0:T(8,128)}, f32[8,128]{1,0:T(8,128)}) custom-call(bf16[768,512]{1,0:T(8,128)(2,1)} %bitcast.9, bf16[768,512]{1,0:T(8,128)(2,1)} %bitcast.10, f32[512]{0:T(512)} %g1_ref.1, ...), custom_call_target="tpu_custom_call" | custom-call | flops 56000000000 | bytes 12000000 | tf_op jit(solution)/shard_map/layer/pallas_call | solution.py:524
  111.1 3.6 %write_out.1 = (bf16[768,512]{1,0:T(8,128)(2,1)}, bf16[768,512]{1,0:T(8,128)(2,1)}, f32[32]{0:T(128)}, f32[32]{0:T(128)}, f32[32]{0:T(128)}, /*index=5*/f32[32]{...) custom-call(bf16[768,512]{1,0:T(8,128)(2,1)} %get-tuple-element.35.o, ...), custom_call_target="tpu_custom_call" | custom-call | tf_op jit(solution)/shard_map/write_out/pallas_call | solution.py:543

commit v9 on v7

--- a/solution.py
+++ b/solution.py
@@ -367,11 +367,11 @@
 
     def arrive(b):
         rows = span(b, NT)
+        for copy in exchange(at, b, buf_ref, z_ref, back_sems):
+            copy.wait()
         if b == NB - 1:
             for s in early:
                 s.step(1)
-        for copy in exchange(at, b, buf_ref, z_ref, back_sems):
-            copy.wait()
         sums_qk, sums_v = [], []
         for p in range(PAIRS):
             seconds = []

time: 112 us -> 113 us (level)
    pallas_call x1, Pallas kernels: 107 us -> 109 us  [device_step(): pl.pallas_call(layer, out_shape=(sds((ROWS, D), BF16), sds((ROWS, D), BF1...]
where the time goes in v9:
time: 113 us
  Pallas kernels  112 us (99%)
    pallas_call x1, Pallas kernels, device_step(): pl.pallas_call(layer, out_shape=(sds((ROWS, D), BF16), sds((ROWS, D), BF1...  109 us
    pallas_call x1, Pallas kernels, device_step(): pl.pallas_call(write_out, out_shape=(tokens, tokens, part, part, part, pa...  3.59 us

profile of v9, /device:TPU:0, one launch (start us, length us, event | category | flops | bytes accessed | tf_op | source)
XLA Modules:
  0.0 113.0 jit_solution(8589958057251329370)
XLA Ops:
  0.7 108.7 %layer.1 = (bf16[768,512]{1,0:T(8,128)(2,1)}, bf16[768,512]{1,0:T(8,128)(2,1)}, f32[32,2048]{1,0:T(8,128)}, f32[128,512]{1,0:T(8,128)}, f32[32,1536]{1,0:T(8,128)}, /*index=5*/f32[32,512]{1,0:T(8,128)}, f32[8,128]{1,0:T(8,128)}) custom-call(bf16[768,512]{1,0:T(8,128)(2,1)} %bitcast.9, bf16[768,512]{1,0:T(8,128)(2,1)} %bitcast.10, f32[512]{0:T(512)} %g1_ref.1, ...), custom_call_target="tpu_custom_call" | custom-call | flops 56000000000 | bytes 12000000 | tf_op jit(solution)/shard_map/layer/pallas_call | solution.py:517
  109.3 3.6 %write_out.1 = (bf16[768,512]{1,0:T(8,128)(2,1)}, bf16[768,512]{1,0:T(8,128)(2,1)}, f32[32]{0:T(128)}, f32[32]{0:T(128)}, f32[32]{0:T(128)}, /*index=5*/f32[32]{...) custom-call(bf16[768,512]{1,0:T(8,128)(2,1)} %get-tuple-element.35.o, ...), custom_call_target="tpu_custom_call" | custom-call | tf_op jit(solution)/shard_map/write_out/pallas_call | solution.py:536
